TPU v7x, 32 devices: a whole 2x2x4 slice. The times are simulated.
32 devices in a mesh: leaf: 8 (over z, y), front: 4 (over x, core).
Axes of the slice: x: 2, y: 2, z: 4, core: 2. Of those that a mesh axis runs over, the one named last changes fastest.
Arguments:
- right_side: float32 [8, 4, 96, 512], P('leaf', 'front'), may hold values from -6 to 6
- factor_inverse: float32 [8, 4, 128, 7680], P('leaf', 'front'), may hold values from -1 to 1, as said below
- update_panel: float32 [8, 4, 128, 1792], P('leaf', 'front'), may hold values from -0.09375 to 0.09375
- update_targets: int32 [8, 14], P('leaf'), may hold values from 0 to 31, as said below
- pivot_pairs: int32 [8, 4, 256], P('leaf', 'front'), may hold values 0 or 1
- pivot_diagonal: float32 [8, 4, 512], P('leaf', 'front'), may hold values from 0.5 to 2
- pivot_coupling: float32 [8, 4, 256], P('leaf', 'front'), may hold values from 3 to 5
Outputs:
- solution: float32 [8, 4, 96, 512], P('leaf', 'front')
Inputs may be any that keep to these rules, and one draw needn't show every extreme that they name: `factor_inverse`: each front's inverse factor is lower triangular in the front's row order with ones on its diagonal. `update_targets`: each front's list names distinct blocks of its parent's pivot rows in rising order, and is repeated in the row of every leaf index of the front's group.
All inputs are finite; a program needn't handle non-finite values. No bound on the sum of `pivot_pairs` on one device may be relied on, other than what follows from the above.
Results may differ from a plain program's by a relative error of at most 0.0001.
Values sent between devices are 32-bit elements; how exact they have to be, the bound alone decides.
A program may use at most 64 MiB of HBM per device.

v0:
```python
import functools

import jax
import jax.numpy as jnp
from jax import lax
from jax.experimental import pallas as pl
from jax.experimental.pallas import tpu as pltpu
from jax.sharding import PartitionSpec as P

LEVELS = 4
BLOCK = 128
MESH = pl.DeviceIdType.MESH
F32 = jnp.float32
BF16 = jnp.bfloat16
PRE_FROM = 1
RELAY_FROM = 1
SHARE = 4


def flip(value, mask):
    result = value
    bit = 0
    while mask >> bit:
        if mask >> bit & 1:
            unit = 1 << bit
            result = result + (1 - 2 * lax.rem(lax.div(value, unit), 2)) * unit
        bit += 1
    return result


def split(values):
    high = values.astype(BF16)
    return high, (values - high.astype(F32)).astype(BF16)


def rows_of(values):
    high, low = split(values)
    return jnp.concatenate([high, low], 0)


def square_of(values):
    high, low = split(values)
    return jnp.concatenate(
        [jnp.concatenate([high, high], 1), jnp.concatenate([low, low], 1)], 0
    )


def along_columns(stacked, matrix):
    return lax.dot_general(
        stacked, matrix, (((1,), (1,)), ((), ())), preferred_element_type=F32
    )


def fold(product, sides, width):
    return (product[:sides, :width] + product[sides:, :width]) + (
        product[:sides, width:] + product[sides:, width:]
    )


def across(square, matrix, sides):
    product = jnp.dot(square, matrix, preferred_element_type=F32)
    return product[:sides] + product[sides:]


class Plan:
    def __init__(self, fronts, sides):
        self.fronts, self.sides = fronts, sides
        half = sides // 2
        self.gathers = {}
        self.scatters = {}
        for level in range(LEVELS):
            self.gathers["rhs", level] = (level, sides)
            self.scatters["out", level] = (level, sides)
        for level in range(LEVELS - 1):
            self.scatters["up", level] = (level, half)
            self.gathers["up", level] = (level + 1, half)
            self.scatters["down", level] = (level + 1, half)
            self.gathers["down", level] = (level, half)

    def size(self, level):
        return self.fronts << level

    def pre(self, key):
        return self.scatters[key][0] >= (1 if key[0] == "out" else PRE_FROM)

    def relay(self, key):
        return self.gathers[key][0] >= (1 if key[0] == "rhs" else RELAY_FROM)


def kernel(plan, pivots, *refs):
    (
        rhs_ref,
        inverse_hbm,
        update_hbm,
        lists_ref,
        pairs_ref,
        diagonal_ref,
        coupling_ref,
        out_ref,
        inverse_raw,
        update_raw,
        inverse_split,
        update_split,
        targets_ref,
        targets_far,
        targets_smem,
        load_sem,
        targets_send,
        targets_recv,
        gather_send,
        gather_recv,
        scatter_send,
        scatter_recv,
        *buffers,
    ) = refs
    sides, fronts = plan.sides, plan.fronts
    half = sides // 2
    nx = fronts // 2
    leaf = lax.axis_index("leaf")
    front = lax.axis_index("front")
    core, column = lax.rem(front, 2), lax.div(front, 2)

    gather_keys = list(plan.gathers)
    scatter_keys = list(plan.scatters)
    gather_buffer, part, landed, first = {}, {}, {}, {}
    buffers = list(buffers)
    for key in gather_keys:
        gather_buffer[key] = buffers.pop(0)
    for key in scatter_keys:
        part[key] = buffers.pop(0)
        landed[key] = buffers.pop(0)
        if plan.pre(key):
            first[key] = buffers.pop(0)

    def rank(level):
        return core * (nx << level) + column * (1 << level) + lax.rem(leaf, 1 << level)

    def peer(level, mask):
        return (
            flip(leaf, mask % (1 << level)),
            flip(column, (mask >> level) % nx) * 2 + flip(core, mask // (nx << level)),
        )

    def slot_block(level, slot):
        slot_core, rest = divmod(slot, nx << level)
        slot_column, offset = divmod(rest, 1 << level)
        return ((slot_column * 2 + slot_core) << level) + offset

    def slot_of(level, block):
        index, offset = divmod(block, 1 << level)
        return (index % 2) * (nx << level) + (index // 2) * (1 << level) + offset

    sends = []

    def send(source, target, send_sem, recv_sem, device):
        pltpu.make_async_remote_copy(
            source, target, send_sem, recv_sem, device_id=device, device_id_type=MESH
        ).start()

    def wait_recv(buffer, count, send_sem, recv_sem):
        span = buffer.at[pl.ds(0, count)]
        pltpu.make_async_remote_copy(
            span, span, send_sem, recv_sem, device_id=peer(0, 1), device_id_type=MESH
        ).wait_recv()

    def wait_send(buffer, count, send_sem, recv_sem):
        span = buffer.at[pl.ds(0, count)]
        pltpu.make_async_remote_copy(
            span, span, send_sem, recv_sem, device_id=peer(0, 1), device_id_type=MESH
        ).wait_send()

    bulk = []

    def issue(count):
        for _ in range(min(count, len(bulk))):
            bulk.pop(0)()

    def far_first(count):
        return sorted(range(1, count), key=lambda mask: -bin(mask).count("1"))

    def gather_start(key, later=False):
        level, _ = plan.gathers[key]
        buffer, index = gather_buffer[key], gather_keys.index(key)
        mine = rank(level)
        sems = gather_send.at[index, 0], gather_recv.at[index, 0]
        count = nx << level if plan.relay(key) else fronts << level
        for mask in far_first(count):

            def one(mask=mask):
                send(buffer.at[mine], buffer.at[mine], *sems, peer(level, mask))

            bulk.append(one) if later else one()
        sends.append((buffer, count - 1, *sems))

    def gather_forward(key):
        level, _ = plan.gathers[key]
        buffer, index = gather_buffer[key], gather_keys.index(key)
        count = nx << level
        if not plan.relay(key):
            return
        wait_recv(buffer, count - 1, gather_send.at[index, 0], gather_recv.at[index, 0])
        span = buffer.at[pl.ds(core * count, count)]
        sems = gather_send.at[index, 1], gather_recv.at[index, 1]
        send(span, span, *sems, peer(level, count))
        sends.append((buffer, count, *sems))

    def gather_finish(key):
        level, _ = plan.gathers[key]
        index = gather_keys.index(key)
        step = 1 if plan.relay(key) else 0
        count = nx << level if step else (fronts << level) - 1
        wait_recv(
            gather_buffer[key], count, gather_send.at[index, step], gather_recv.at[index, step]
        )

    def scatter_start(key):
        level, _ = plan.scatters[key]
        index = scatter_keys.index(key)
        count = nx << level
        if plan.pre(key):
            sems = scatter_send.at[index, 0], scatter_recv.at[index, 0]
            send(
                part[key].at[pl.ds((1 - core) * count, count)], first[key], *sems, peer(level, count)
            )
            sends.append((part[key], count, *sems))
        else:
            scatter_spread(key, 2 * count)

    def scatter_spread(key, count, later=False):
        level, _ = plan.scatters[key]
        index = scatter_keys.index(key)
        mine = rank(level)
        sems = scatter_send.at[index, 1], scatter_recv.at[index, 1]
        for mask in far_first(count):

            def one(mask=mask):
                send(
                    part[key].at[flip(mine, mask)],
                    landed[key].at[mask - 1],
                    *sems,
                    peer(level, mask),
                )

            bulk.append(one) if later else one()
        sends.append((part[key], count - 1, *sems))

    def scatter_middle(key, later=False):
        level, _ = plan.scatters[key]
        index = scatter_keys.index(key)
        count = nx << level
        if plan.pre(key):
            wait_recv(first[key], count, scatter_send.at[index, 0], scatter_recv.at[index, 0])
            span = pl.ds(core * count, count)
            part[key][span] = part[key][span] + first[key][...]
            scatter_spread(key, count, later)

    def scatter_finish(key):
        level, _ = plan.scatters[key]
        index = scatter_keys.index(key)
        count = (nx << level) if plan.pre(key) else fronts << level
        wait_recv(landed[key], count - 1, scatter_send.at[index, 1], scatter_recv.at[index, 1])
        total = part[key][rank(level)]
        for place in range(count - 1):
            total = total + landed[key][place]
        return total

    def column_start(level):
        return fronts * pivots * ((1 << level) - 1)

    def update_start(level):
        return 2 * pivots * ((1 << level) - 1)

    loads = []
    for level in range(LEVELS):
        cols = pl.ds(column_start(level), (fronts * pivots) << level)
        loads.append(
            pltpu.make_async_copy(
                inverse_hbm.at[0, 0, :, cols], inverse_raw.at[:, cols], load_sem.at[level]
            )
        )
    loads.append(pltpu.make_async_copy(update_hbm.at[0, 0], update_raw, load_sem.at[LEVELS]))
    loads[0].start()
    loads[LEVELS].start()
    for level in range(1, LEVELS):
        loads[level].start()

    for level in range(LEVELS):
        gather_buffer["rhs", level][rank(level)] = rhs_ref[
            0, 0, :, level * pivots : (level + 1) * pivots
        ]

    targets_ref[...] = jnp.zeros_like(targets_ref)
    targets_ref[:1, : lists_ref.shape[1]] = lists_ref[...]

    barrier = pltpu.get_barrier_semaphore()
    everyone = plan.size(LEVELS - 1)
    for mask in range(1, everyone):
        pl.semaphore_signal(
            barrier, inc=1, device_id=peer(LEVELS - 1, mask), device_id_type=MESH
        )
    pl.semaphore_wait(barrier, everyone - 1)

    gather_start(("rhs", 0))
    for level in range(LEVELS - 1):
        send(
            targets_ref,
            targets_far.at[level],
            targets_send.at[level],
            targets_recv.at[level],
            (flip(leaf, 1 << level), front),
        )
    gather_start(("rhs", 1))

    def prepare(level):
        loads[level].wait()
        for block in range(column_start(level) // BLOCK, column_start(level + 1) // BLOCK):
            high, low = split(inverse_raw[:, block * BLOCK : (block + 1) * BLOCK])
            inverse_split[block, :pivots] = high
            inverse_split[block, pivots:] = low

    def inverse_columns(start, stop):
        blocks = range(start // BLOCK, stop // BLOCK)
        return jnp.concatenate([inverse_split[block] for block in blocks], 1)

    def prepare_update(level):
        cols = slice(update_start(level), update_start(level + 1))
        high, low = split(update_raw[:, cols])
        update_split[:pivots, cols] = high
        update_split[pivots:, cols] = low

    for level in range(2, LEVELS):
        gather_start(("rhs", level), later=True)
    issue(SHARE)
    prepare(0)
    loads[LEVELS].wait()
    prepare_update(0)

    def swap(values):
        width = values.shape[1]
        even = lax.rem(lax.broadcasted_iota(jnp.int32, values.shape, 1), 2) == 0
        return jnp.where(
            even, pltpu.roll(values, width - 1, 1), pltpu.roll(values, 1, 1)
        )

    def pivot_coefficients():
        width = diagonal_ref.shape[2]
        from_pair = (
            lax.div(lax.broadcasted_iota(jnp.int32, (width // 2, width), 1), 2)
            == lax.broadcasted_iota(jnp.int32, (width // 2, width), 0)
        ).astype(F32)
        pair_rows = jnp.concatenate(
            [
                jnp.broadcast_to(coupling_ref[0], (8, width // 2)),
                jnp.broadcast_to(pairs_ref[0].astype(F32), (8, width // 2)),
            ],
            0,
        )
        repeated = jnp.dot(
            pair_rows, from_pair, precision=lax.Precision.HIGHEST, preferred_element_type=F32
        )
        couple, flags = repeated[:8], repeated[8:] > 0.5
        diagonal = jnp.broadcast_to(diagonal_ref[0], (8, width))

        other_diagonal = swap(diagonal)
        determinant = diagonal * other_diagonal - couple * couple
        straight = jnp.where(flags, other_diagonal / determinant, 1.0 / diagonal)[:1]
        crossed = jnp.where(flags, -couple / determinant, 0.0)[:1]
        return straight, crossed

    def pivot_solve(solved, level, straight, crossed):
        span = slice(level * pivots, (level + 1) * pivots)
        return solved * straight[:, span] + swap(solved) * crossed[:, span]

    def fetch_lists():
        for level in range(LEVELS - 1):
            pltpu.make_async_remote_copy(
                targets_ref,
                targets_far.at[level],
                targets_send.at[level],
                targets_recv.at[level],
                device_id=(flip(leaf, 1 << level), front),
                device_id_type=MESH,
            ).wait()
        lists = [targets_ref] + [targets_far.at[level] for level in range(LEVELS - 1)]
        copies = [
            pltpu.make_async_copy(source, targets_smem.at[index], load_sem.at[LEVELS + 1 + index])
            for index, source in enumerate(lists)
        ]
        for copy in copies:
            copy.start()
        for copy in copies:
            copy.wait()

    def block_count(level):
        return 2 * pivots * (1 << level) // BLOCK

    def chosen_columns(level, child, index):
        place = update_start(level) // BLOCK + index
        upper = lax.rem(lax.div(leaf, 1 << level), 2)
        near, far = targets_smem[0, 0, place], targets_smem[level + 1, 0, place]
        block = near + (far - near) * (upper + child - 2 * upper * child)
        return inverse_split[column_start(level + 1) // BLOCK + block]

    def known_part(level):
        buffer = gather_buffer["rhs", level]
        product = None
        step = 2 if level else 1
        for slot in range(0, plan.size(level), step):
            start = column_start(level) + slot_block(level, slot) * pivots
            values = jnp.concatenate([buffer[slot + i] for i in range(step)], 1)
            term = along_columns(
                rows_of(values), inverse_columns(start, start + step * pivots)
            )
            product = term if product is None else product + term
        return product

    def block_at(buffer, level, child, index, parent):
        halves = []
        for place in (2 * index, 2 * index + 1):
            slot = slot_of(level, place)
            if parent:
                rank_core, rest = divmod(slot, nx << level)
                rank_column, offset = divmod(rest, 1 << level)
                slot = (
                    rank_core * (nx << (level + 1))
                    + rank_column * (1 << (level + 1))
                    + (child << level)
                    + offset
                )
            halves.append(slot)
        return halves

    weighted = []
    gather_finish(("rhs", 0))
    product = known_part(0)
    for level in range(LEVELS):
        if level:
            below = level - 1
            key = ("up", below)
            gather_finish(key)
            buffer = gather_buffer[key]
            for child in range(2):
                for index in range(0, block_count(below), 2):
                    values, matrices = [], []
                    for i in (index, index + 1):
                        low_slot, high_slot = block_at(buffer, below, child, i, True)
                        values.append(
                            jnp.concatenate([buffer[low_slot], buffer[high_slot]], 0)
                        )
                        matrices.append(chosen_columns(below, child, i))
                    product = product - along_columns(
                        rows_of(jnp.concatenate(values, 1)), jnp.concatenate(matrices, 1)
                    )
        solved = fold(product, sides, pivots)
        if level + 1 < LEVELS:
            key = ("up", level)
            start = update_start(level)
            blocks = block_count(level)
            partial = across(
                square_of(solved), update_split[:, start : start + blocks * BLOCK], sides
            )
            for index in range(blocks):
                for i, slot in enumerate(block_at(None, level, 0, index, False)):
                    part[key][slot] = partial[
                        i * half : (i + 1) * half, index * BLOCK : (index + 1) * BLOCK
                    ]
            scatter_start(key)
            issue(SHARE)
            if level == 0:
                coefficients = pivot_coefficients()
            weighted.append(pivot_solve(solved, level, *coefficients))
            scatter_middle(key)
            if plan.pre(key):
                issue(SHARE)
            prepare(level + 1)
            if level + 2 < LEVELS:
                prepare_update(level + 1)
            if level == 0:
                fetch_lists()
            if level + 2 == LEVELS:
                issue(len(bulk))
            gather_forward(("rhs", level + 1))
            total = scatter_finish(key)
            gather_buffer[key][rank(level + 1)] = total
            gather_start(key)
            issue(SHARE)
            gather_finish(("rhs", level + 1))
            product = known_part(level + 1)
            gather_forward(key)
            issue(SHARE)
        else:
            weighted.append(pivot_solve(solved, level, *coefficients))

    for level in reversed(range(LEVELS)):
        target = weighted[level]
        if level + 1 < LEVELS:
            key = ("down", level)
            gather_finish(key)
            buffer = gather_buffer[key]
            product = None
            for index in range(0, block_count(level), 2):
                values = []
                for i in (index, index + 1):
                    low_slot, high_slot = block_at(buffer, level, 0, i, False)
                    values.append(jnp.concatenate([buffer[low_slot], buffer[high_slot]], 0))
                start = update_start(level) + index * BLOCK
                term = along_columns(
                    rows_of(jnp.concatenate(values, 1)),
                    update_split[:, start : start + 2 * BLOCK],
                )
                product = term if product is None else product + term
            target = target - fold(product, sides, pivots)
        square = square_of(target)
        if level:
            key = ("down", level - 1)
            for child in range(2):
                for index in range(0, block_count(level - 1), 2):
                    matrix = jnp.concatenate(
                        [chosen_columns(level - 1, child, i) for i in (index, index + 1)], 1
                    )
                    partial = across(square, matrix, sides)
                    for j in range(2):
                        places = block_at(None, level - 1, child, index + j, True)
                        for i, slot in enumerate(places):
                            part[key][slot] = partial[
                                i * half : (i + 1) * half, j * BLOCK : (j + 1) * BLOCK
                            ]
            scatter_start(key)
            scatter_middle(key)
            issue(SHARE)
        out_key = ("out", level)
        step = 2 if level else 1
        for slot in range(0, plan.size(level), step):
            start = column_start(level) + slot_block(level, slot) * pivots
            partial = across(square, inverse_columns(start, start + step * pivots), sides)
            for i in range(step):
                part[out_key][slot + i] = partial[:, i * pivots : (i + 1) * pivots]
        scatter_start(out_key)
        if level:
            total = scatter_finish(key)
            gather_buffer[key][rank(level - 1)] = total
            gather_start(key)
            scatter_middle(out_key, later=True)
            issue(SHARE)
            gather_forward(key)
            issue(SHARE)
    issue(len(bulk))
    for level in reversed(range(LEVELS)):
        out_ref[0, 0, :, level * pivots : (level + 1) * pivots] = scatter_finish(("out", level))
    for item in sends:
        wait_send(*item)


def per_device(*arguments):
    (
        right_side,
        factor_inverse,
        update_panel,
        update_targets,
        pivot_pairs,
        pivot_diagonal,
        pivot_coupling,
    ) = arguments
    pivots = factor_inverse.shape[2]
    sides = right_side.shape[2]
    fronts = lax.axis_size("front")
    plan = Plan(fronts, sides)
    nx = fronts // 2
    targets = jax.ShapeDtypeStruct((8, BLOCK), jnp.int32)
    buffers = []
    for level, rows in plan.gathers.values():
        buffers.append(pltpu.VMEM((plan.size(level), rows, pivots), F32))
    for key, (level, rows) in plan.scatters.items():
        buffers.append(pltpu.VMEM((plan.size(level), rows, pivots), F32))
        buffers.append(pltpu.VMEM((plan.size(level), rows, pivots), F32))
        if plan.pre(key):
            buffers.append(pltpu.VMEM((nx << level, rows, pivots), F32))
    vmem = pl.BlockSpec(memory_space=pltpu.VMEM)
    hbm = pl.BlockSpec(memory_space=pl.ANY)
    dma = pltpu.SemaphoreType.DMA
    return pl.pallas_call(
        functools.partial(kernel, plan, pivots),
        out_shape=jax.ShapeDtypeStruct(right_side.shape, F32),
        in_specs=[vmem, hbm, hbm, vmem, vmem, vmem, vmem],
        out_specs=vmem,
        scratch_shapes=[
            pltpu.VMEM(factor_inverse.shape[2:], F32),
            pltpu.VMEM(update_panel.shape[2:], F32),
            pltpu.VMEM((factor_inverse.shape[3] // BLOCK, 2 * pivots, BLOCK), BF16),
            pltpu.VMEM((2 * pivots, update_panel.shape[3]), BF16),
            pltpu.VMEM(targets.shape, jnp.int32),
            pltpu.VMEM((LEVELS - 1,) + targets.shape, jnp.int32),
            pltpu.SMEM((LEVELS,) + targets.shape, jnp.int32),
            dma((2 * LEVELS + 1,)),
            dma((LEVELS - 1,)),
            dma((LEVELS - 1,)),
            dma((len(plan.gathers), 2)),
            dma((len(plan.gathers), 2)),
            dma((len(plan.scatters), 2)),
            dma((len(plan.scatters), 2)),
            *buffers,
        ],
        compiler_params=pltpu.CompilerParams(collective_id=0, has_side_effects=True),
    )(
        right_side,
        factor_inverse,
        update_panel,
        update_targets,
        pivot_pairs,
        pivot_diagonal,
        pivot_coupling,
    )


def solution(mesh):
    in_specs = (
        P("leaf", "front", None, None),
        P("leaf", "front", None, None),
        P("leaf", "front", None, None),
        P("leaf", None),
        P("leaf", "front", None),
        P("leaf", "front", None),
        P("leaf", "front", None),
    )
    out_specs = P("leaf", "front", None, None)
    return jax.shard_map(
        per_device, mesh=mesh, in_specs=in_specs, out_specs=out_specs, check_vma=False
    )
```

profile of v0, /device:TPU:0, one launch (start us, length us, event | category | flops | bytes accessed | tf_op | source)
XLA Modules:
  0.0 102.5 jit_solution(785204202912397555)
XLA Ops:
  0.0 100.9 %shard_map.73 = f32[1,1,96,512]{3,2,1,0:T(8,128)} custom-call(f32[1,1,96,512]{3,2,1,0:T(8,128)} %refs_0_.1, f32[1,1,128,7680]{3,2,1,0:T(8,128)} %refs_1_.1, f32[1,1,128,1792]{3,2,1,0:T(8,128)} %refs_2_.1, s32[1,14]{1,0:T(1,128)} %refs_3_.1, s32[1,1,256]{2,1,0:T(1,128)} %refs_4_.1, f32[1,1,512]{2,1,0:T(1,128)} %refs_5_.1, f32[1,1,256]{2,1,0:T(1,128)} %refs_6_.1), custom_call_target="tpu_custom_call" | custom-call | tf_op jit(solution)/shard_map/pallas_call | solution.py:581
  100.9 1.6 %copy.9 = f32[1,1,96,512]{3,2,1,0:T(8,128)} copy(f32[1,1,96,512]{3,2,1,0:T(8,128)} %shard_map.73) | data formatting | bytes 393216
where the time goes:
time: 103 us; the launch traced here: 102 us
  Pallas kernels  101 us (98%)
  local copies, waits for them, and re-layouts  1.62 us (2%)
    pallas_call x1, Pallas kernels, per_device(): pl.pallas_call(functools.partial(kernel, plan, pivots), out_shape=jax.Sha...  101 us

commit v1 on v0

--- a/solution.py
+++ b/solution.py
@@ -111,6 +111,21 @@
         gather_recv,
         scatter_send,
         scatter_recv,
+        rhs_send,
+        rhs_recv,
+        side_send,
+        side_recv,
+        cross_part,
+        cross_first,
+        cross_landed,
+        cross_row,
+        cross_col,
+        cross_row_split,
+        cross_col_split,
+        low_part,
+        low_first,
+        low_landed,
+        low_split,
         *buffers,
     ) = refs
     sides, fronts = plan.sides, plan.fronts
@@ -147,8 +162,32 @@
         return ((slot_column * 2 + slot_core) << level) + offset
 
     def slot_of(level, block):
-        index, offset = divmod(block, 1 << level)
-        return (index % 2) * (nx << level) + (index // 2) * (1 << level) + offset
+        index, part_of = divmod(block, 2)
+        return part_of * (nx << level) + index
+
+    def rhs_slot(level):
+        if not level:
+            return rank(0)
+        inside = lax.rem(leaf, 1 << level)
+        if level == LEVELS - 1:
+            depth = 1 << level - 1
+            run = (core * 2 + lax.rem(inside, 2)) * nx + column
+            return run * depth + lax.div(inside, 2)
+        return (
+            core * (nx << level) + lax.div(inside, 2) * (2 * nx) + column * 2 + lax.rem(inside, 2)
+        )
+
+    def rhs_block(level, slot):
+        if not level:
+            return slot_block(0, slot)
+        slot_core, rest = divmod(slot, nx << level)
+        if level == LEVELS - 1:
+            rest, deep = divmod(rest, 1 << level - 1)
+            row, slot_column = divmod(rest, nx)
+            return ((slot_column * 2 + slot_core) << level) + deep * 2 + row
+        deep, rest = divmod(rest, 2 * nx)
+        slot_column, row = divmod(rest, 2)
+        return ((slot_column * 2 + slot_core) << level) + deep * 2 + row
 
     sends = []
 
@@ -212,6 +251,152 @@
         wait_recv(
             gather_buffer[key], count, gather_send.at[index, step], gather_recv.at[index, step]
         )
+
+    def rhs_sems(level, phase):
+        return rhs_send.at[level, phase], rhs_recv.at[level, phase]
+
+    def for_column(body):
+        for index in range(nx):
+
+            @pl.when(column == index)
+            def _():
+                body(index)
+
+    def rhs_across(level):
+        @pl.when(column == 0)
+        def _():
+            slot = gather_buffer["rhs", level].at[rhs_slot(level)]
+            send(slot, slot, *rhs_sems(level, 0), peer(level, 1 << level))
+
+    def rhs_beside(level):
+        buffer = gather_buffer["rhs", level]
+
+        def body(index):
+            if index:
+                wait_recv(buffer, index, *rhs_sems(level, 0))
+            for back in range(index + 1):
+                slot = buffer.at[rhs_slot(level) - 2 * back]
+                send(slot, slot, *rhs_sems(level, 1), peer(level, 1))
+
+        for_column(body)
+
+    def rhs_deep(level):
+        buffer, depth = gather_buffer["rhs", level], 1 << level - 1
+        start = core * (nx << level) + lax.div(lax.rem(leaf, 1 << level), 2) * (2 * nx)
+
+        def body(index):
+            wait_recv(buffer, index + 1, *rhs_sems(level, 1))
+            span = buffer.at[pl.ds(start, 2 * (index + 1))]
+            for deep in range(1, depth):
+                send(span, span, *rhs_sems(level, 2), peer(level, 2 * deep))
+
+        for_column(body)
+
+    top = LEVELS - 1
+    top_depth = 1 << top - 1
+
+    def top_run(row, slot_column):
+        start = ((core * 2 + row) * nx + slot_column) * top_depth
+        return gather_buffer["rhs", top].at[pl.ds(start, top_depth)]
+
+    def top_deep():
+        slot = gather_buffer["rhs", top].at[rhs_slot(top)]
+        for deep in range(top_depth - 1, 0, -1):
+            send(slot, slot, *rhs_sems(top, 0), peer(top, 2 * deep))
+        sends.append((gather_buffer["rhs", top], top_depth - 1, *rhs_sems(top, 0)))
+
+    def top_first():
+        row = lax.rem(leaf, 2)
+        wait_recv(gather_buffer["rhs", top], top_depth - 1, *rhs_sems(top, 0))
+        run = top_run(row, column)
+        send(run, run, *rhs_sems(top, 2), peer(top, 1))
+        sends.append((gather_buffer["rhs", top], top_depth, *rhs_sems(top, 2)))
+
+        @pl.when((column == 0) & (core == 0))
+        def _():
+            span = top_run(row, 0)
+            send(span, span, *rhs_sems(top, 1), peer(top, 1 << top))
+
+    def top_second():
+        row = lax.rem(leaf, 2)
+        buffer = gather_buffer["rhs", top]
+
+        @pl.when((column == 0) & (core == 1))
+        def _():
+            wait_recv(buffer, top_depth, *rhs_sems(top, 2))
+            for each in range(2):
+                span = top_run(each, 0)
+                send(span, span, *rhs_sems(top, 1), peer(top, 1 << top))
+
+        @pl.when((column == 1) & (core == 0))
+        def _():
+            wait_recv(buffer, top_depth, *rhs_sems(top, 1))
+            span = top_run(row, 0)
+            send(span, span, *rhs_sems(top, 2), peer(top, 1))
+
+    def top_relay():
+        buffer = gather_buffer["rhs", top]
+
+        @pl.when((column == 0) & (core == 0))
+        def _():
+            wait_recv(buffer, top_depth, *rhs_sems(top, 2))
+
+        @pl.when((column == 1) & (core == 0))
+        def _():
+            wait_recv(buffer, 2 * top_depth, *rhs_sems(top, 2))
+
+        @pl.when((column == 1) & (core == 1))
+        def _():
+            wait_recv(buffer, top_depth, *rhs_sems(top, 2))
+            wait_recv(buffer, 2 * top_depth, *rhs_sems(top, 1))
+
+        span = buffer.at[pl.ds(core * (nx << top), nx << top)]
+        send(span, span, *rhs_sems(top, 3), peer(top, nx << top))
+        sends.append((buffer, nx << top, *rhs_sems(top, 3)))
+
+    def top_drain():
+        buffer = gather_buffer["rhs", top]
+
+        @pl.when((column == 0) & (core == 0))
+        def _():
+            wait_send(buffer, top_depth, *rhs_sems(top, 1))
+
+        @pl.when((column == 0) & (core == 1))
+        def _():
+            wait_send(buffer, 2 * top_depth, *rhs_sems(top, 1))
+
+        @pl.when((column == 1) & (core == 0))
+        def _():
+            wait_send(buffer, top_depth, *rhs_sems(top, 2))
+
+    def rhs_relay(level):
+        buffer, depth = gather_buffer["rhs", level], 1 << level - 1
+
+        def body(index):
+            if depth > 1:
+                wait_recv(buffer, 2 * (depth - 1) * (index + 1), *rhs_sems(level, 2))
+            else:
+                wait_recv(buffer, index + 1, *rhs_sems(level, 1))
+
+        for_column(body)
+        span = buffer.at[pl.ds(core * (nx << level), nx << level)]
+        send(span, span, *rhs_sems(level, 3), peer(level, nx << level))
+        sends.append((buffer, nx << level, *rhs_sems(level, 3)))
+
+    def rhs_finish(level):
+        wait_recv(gather_buffer["rhs", level], nx << level, *rhs_sems(level, 3))
+
+    def rhs_drain(level):
+        buffer, depth = gather_buffer["rhs", level], 1 << level - 1
+
+        def body(index):
+            if not index:
+                wait_send(buffer, 1, *rhs_sems(level, 0))
+            wait_send(buffer, index + 1, *rhs_sems(level, 1))
+            if depth > 1:
+                wait_send(buffer, 2 * (depth - 1) * (index + 1), *rhs_sems(level, 2))
+
+        for_column(body)
 
     def scatter_start(key):
         level, _ = plan.scatters[key]
@@ -285,9 +470,16 @@
         loads[level].start()
 
     for level in range(LEVELS):
-        gather_buffer["rhs", level][rank(level)] = rhs_ref[
+        gather_buffer["rhs", level][rhs_slot(level)] = rhs_ref[
             0, 0, :, level * pivots : (level + 1) * pivots
         ]
+
+    @pl.when(column == 0)
+    def _():
+        for level in range(1, LEVELS):
+            for slot in range(plan.size(level)):
+                if rhs_block(level, slot) >> level >= 2:
+                    gather_buffer["rhs", level][slot] = jnp.zeros((sides, pivots), F32)
 
     targets_ref[...] = jnp.zeros_like(targets_ref)
     targets_ref[:1, : lists_ref.shape[1]] = lists_ref[...]
@@ -300,7 +492,6 @@
         )
     pl.semaphore_wait(barrier, everyone - 1)
 
-    gather_start(("rhs", 0))
     for level in range(LEVELS - 1):
         send(
             targets_ref,
@@ -309,7 +500,10 @@
             targets_recv.at[level],
             (flip(leaf, 1 << level), front),
         )
-    gather_start(("rhs", 1))
+    gather_start(("rhs", 0))
+    for level in range(1, top):
+        rhs_across(level)
+    top_deep()
 
     def prepare(level):
         loads[level].wait()
@@ -328,9 +522,6 @@
         update_split[:pivots, cols] = high
         update_split[pivots:, cols] = low
 
-    for level in range(2, LEVELS):
-        gather_start(("rhs", level), later=True)
-    issue(SHARE)
     prepare(0)
     loads[LEVELS].wait()
     prepare_update(0)
@@ -371,8 +562,8 @@
         span = slice(level * pivots, (level + 1) * pivots)
         return solved * straight[:, span] + swap(solved) * crossed[:, span]
 
-    def fetch_lists():
-        for level in range(LEVELS - 1):
+    def fetch_lists(levels, own):
+        for level in levels:
             pltpu.make_async_remote_copy(
                 targets_ref,
                 targets_far.at[level],
@@ -381,10 +572,11 @@
                 device_id=(flip(leaf, 1 << level), front),
                 device_id_type=MESH,
             ).wait()
-        lists = [targets_ref] + [targets_far.at[level] for level in range(LEVELS - 1)]
+        lists = [(targets_ref, 0)] if own else []
+        lists += [(targets_far.at[level], level + 1) for level in levels]
         copies = [
             pltpu.make_async_copy(source, targets_smem.at[index], load_sem.at[LEVELS + 1 + index])
-            for index, source in enumerate(lists)
+            for source, index in lists
         ]
         for copy in copies:
             copy.start()
@@ -406,10 +598,12 @@
         product = None
         step = 2 if level else 1
         for slot in range(0, plan.size(level), step):
-            start = column_start(level) + slot_block(level, slot) * pivots
             values = jnp.concatenate([buffer[slot + i] for i in range(step)], 1)
+            first_block = column_start(level) // BLOCK
+            blocks = [first_block + rhs_block(level, slot + i) for i in range(step)]
             term = along_columns(
-                rows_of(values), inverse_columns(start, start + step * pivots)
+                rows_of(values),
+                jnp.concatenate([inverse_split[block] for block in blocks], 1),
             )
             product = term if product is None else product + term
         return product
@@ -430,104 +624,159 @@
             halves.append(slot)
         return halves
 
-    weighted = []
-    gather_finish(("rhs", 0))
-    product = known_part(0)
-    for level in range(LEVELS):
-        if level:
-            below = level - 1
-            key = ("up", below)
-            gather_finish(key)
-            buffer = gather_buffer[key]
-            for child in range(2):
-                for index in range(0, block_count(below), 2):
-                    values, matrices = [], []
-                    for i in (index, index + 1):
-                        low_slot, high_slot = block_at(buffer, below, child, i, True)
-                        values.append(
-                            jnp.concatenate([buffer[low_slot], buffer[high_slot]], 0)
-                        )
-                        matrices.append(chosen_columns(below, child, i))
-                    product = product - along_columns(
-                        rows_of(jnp.concatenate(values, 1)), jnp.concatenate(matrices, 1)
-                    )
-        solved = fold(product, sides, pivots)
-        if level + 1 < LEVELS:
-            key = ("up", level)
-            start = update_start(level)
-            blocks = block_count(level)
-            partial = across(
-                square_of(solved), update_split[:, start : start + blocks * BLOCK], sides
+    group, wide = nx << 1, nx
+    corner = column * 2 + lax.rem(leaf, 2)
+    pair_mask = group
+
+    def side(index):
+        return side_send.at[index], side_recv.at[index]
+
+    def turned(level):
+        cols = slice(update_start(level), update_start(level + 1))
+        high, low = split(update_raw[:, cols].T)
+        return jnp.concatenate(
+            [jnp.concatenate([high, low], 1), jnp.concatenate([low, high], 1)], 0
+        )
+
+    def cross_start():
+        left = turned(1)
+        rows = left.shape[0] // 2
+        for half_index in range(2):
+            picks = []
+            for i in range(wide):
+                index, child = divmod(half_index * wide + i, 2)
+                picks.append(chosen_columns(0, child, index))
+            product = across(left, jnp.concatenate(picks, 1), rows)
+            for block in range(group):
+                for i in range(wide):
+                    cross_part[half_index, block, i] = product[
+                        block * pivots : (block + 1) * pivots, i * pivots : (i + 1) * pivots
+                    ]
+        send(cross_part.at[1 - core], cross_first, *side(0), peer(1, pair_mask))
+        sends.append((cross_first, group, *side(0)))
+
+    def cross_spread():
+        wait_recv(cross_first, group, *side(0))
+        for block in range(group):
+            cross_part[core, block] = cross_part[core, block] + cross_first[block]
+        for mask in far_first(group):
+            send(
+                cross_part.at[core, flip(corner, mask)],
+                cross_landed.at[mask - 1],
+                *side(1),
+                peer(1, mask),
             )
-            for index in range(blocks):
-                for i, slot in enumerate(block_at(None, level, 0, index, False)):
-                    part[key][slot] = partial[
-                        i * half : (i + 1) * half, index * BLOCK : (index + 1) * BLOCK
-                    ]
-            scatter_start(key)
-            issue(SHARE)
-            if level == 0:
-                coefficients = pivot_coefficients()
-            weighted.append(pivot_solve(solved, level, *coefficients))
-            scatter_middle(key)
-            if plan.pre(key):
-                issue(SHARE)
-            prepare(level + 1)
-            if level + 2 < LEVELS:
-                prepare_update(level + 1)
-            if level == 0:
-                fetch_lists()
-            if level + 2 == LEVELS:
-                issue(len(bulk))
-            gather_forward(("rhs", level + 1))
-            total = scatter_finish(key)
-            gather_buffer[key][rank(level + 1)] = total
-            gather_start(key)
-            issue(SHARE)
-            gather_finish(("rhs", level + 1))
-            product = known_part(level + 1)
-            gather_forward(key)
-            issue(SHARE)
-        else:
-            weighted.append(pivot_solve(solved, level, *coefficients))
-
-    for level in reversed(range(LEVELS)):
-        target = weighted[level]
-        if level + 1 < LEVELS:
-            key = ("down", level)
-            gather_finish(key)
-            buffer = gather_buffer[key]
-            product = None
-            for index in range(0, block_count(level), 2):
-                values = []
+        sends.append((cross_landed, group - 1, *side(1)))
+
+    def cross_share():
+        wait_recv(cross_landed, group - 1, *side(1))
+        total = cross_part[core, corner]
+        for place in range(group - 1):
+            total = total + cross_landed[place]
+        span = cross_row.at[pl.ds(core * wide, wide)]
+        cross_row[pl.ds(core * wide, wide)] = total
+        send(span, span, *side(2), peer(1, pair_mask))
+        sends.append((cross_row, wide, *side(2)))
+
+    def cross_rows():
+        wait_recv(cross_row, wide, *side(2))
+        for block in range(group):
+            cols = slice(block * pivots, (block + 1) * pivots)
+            high, low = split(cross_row[block])
+            cross_row_split[:pivots, cols] = high
+            cross_row_split[pivots:, cols] = low
+
+    def cross_turn():
+        for mask in far_first(group):
+            send(
+                cross_row.at[flip(corner, mask)], cross_col.at[corner], *side(3), peer(1, mask)
+            )
+        sends.append((cross_row, group - 1, *side(3)))
+        cross_col[corner] = cross_row[corner]
+
+    def cross_columns():
+        wait_recv(cross_col, group - 1, *side(3))
+        for block in range(group):
+            high, low = split(cross_col[block])
+            cross_col_split[block, :pivots] = high
+            cross_col_split[block, pivots:] = low
+
+    def low_start():
+        left = turned(0)
+        rows = left.shape[0] // 2
+        for target in range(fronts):
+            product = across(left, inverse_split[target], rows)
+            for i in range(nx):
+                low_part[target % 2, target // 2, i] = product[i * pivots : (i + 1) * pivots]
+        send(low_part.at[1 - core], low_first, *side(4), peer(0, nx))
+        sends.append((low_first, nx, *side(4)))
+
+    def low_spread():
+        wait_recv(low_first, nx, *side(4))
+        for target in range(nx):
+            low_part[core, target] = low_part[core, target] + low_first[target]
+        for mask in range(1, nx):
+            send(
+                low_part.at[core, flip(column, mask)], low_landed.at[mask - 1], *side(5), peer(0, mask)
+            )
+        sends.append((low_landed, nx - 1, *side(5)))
+
+    def low_finish():
+        wait_recv(low_landed, nx - 1, *side(5))
+        total = low_part[core, column]
+        for place in range(nx - 1):
+            total = total + low_landed[place]
+        for i in range(nx):
+            high, low = split(total[i])
+            low_split[i, :pivots] = high
+            low_split[i, pivots:] = low
+
+    def sent_up(solved, level):
+        key = ("up", level)
+        start = update_start(level)
+        blocks = block_count(level)
+        partial = across(
+            square_of(solved), update_split[:, start : start + blocks * BLOCK], sides
+        )
+        for index in range(blocks):
+            for i, slot in enumerate(block_at(None, level, 0, index, False)):
+                part[key][slot] = partial[
+                    i * half : (i + 1) * half, index * BLOCK : (index + 1) * BLOCK
+                ]
+        scatter_start(key)
+
+    def less_children(product, level):
+        below = level - 1
+        buffer = gather_buffer["up", below]
+        for child in range(2):
+            for index in range(0, block_count(below), 2):
+                values, matrices = [], []
                 for i in (index, index + 1):
-                    low_slot, high_slot = block_at(buffer, level, 0, i, False)
+                    low_slot, high_slot = block_at(buffer, below, child, i, True)
                     values.append(jnp.concatenate([buffer[low_slot], buffer[high_slot]], 0))
-                start = update_start(level) + index * BLOCK
-                term = along_columns(
-                    rows_of(jnp.concatenate(values, 1)),
-                    update_split[:, start : start + 2 * BLOCK],
+                    matrices.append(chosen_columns(below, child, i))
+                product = product - along_columns(
+                    rows_of(jnp.concatenate(values, 1)), jnp.concatenate(matrices, 1)
                 )
-                product = term if product is None else product + term
-            target = target - fold(product, sides, pivots)
-        square = square_of(target)
-        if level:
-            key = ("down", level - 1)
-            for child in range(2):
-                for index in range(0, block_count(level - 1), 2):
-                    matrix = jnp.concatenate(
-                        [chosen_columns(level - 1, child, i) for i in (index, index + 1)], 1
-                    )
-                    partial = across(square, matrix, sides)
-                    for j in range(2):
-                        places = block_at(None, level - 1, child, index + j, True)
-                        for i, slot in enumerate(places):
-                            part[key][slot] = partial[
-                                i * half : (i + 1) * half, j * BLOCK : (j + 1) * BLOCK
-                            ]
-            scatter_start(key)
-            scatter_middle(key)
-            issue(SHARE)
+        return product
+
+    def sent_down(square, level):
+        key = ("down", level - 1)
+        for child in range(2):
+            for index in range(0, block_count(level - 1), 2):
+                matrix = jnp.concatenate(
+                    [chosen_columns(level - 1, child, i) for i in (index, index + 1)], 1
+                )
+                partial = across(square, matrix, sides)
+                for j in range(2):
+                    places = block_at(None, level - 1, child, index + j, True)
+                    for i, slot in enumerate(places):
+                        part[key][slot] = partial[
+                            i * half : (i + 1) * half, j * BLOCK : (j + 1) * BLOCK
+                        ]
+        scatter_start(key)
+
+    def sent_out(square, level):
         out_key = ("out", level)
         step = 2 if level else 1
         for slot in range(0, plan.size(level), step):
@@ -536,19 +785,150 @@
             for i in range(step):
                 part[out_key][slot + i] = partial[:, i * pivots : (i + 1) * pivots]
         scatter_start(out_key)
-        if level:
+
+    def with_parent(level):
+        buffer = gather_buffer["down", level]
+        product = None
+        for index in range(0, block_count(level), 2):
+            values = []
+            for i in (index, index + 1):
+                low_slot, high_slot = block_at(buffer, level, 0, i, False)
+                values.append(jnp.concatenate([buffer[low_slot], buffer[high_slot]], 0))
+            start = update_start(level) + index * BLOCK
+            term = along_columns(
+                rows_of(jnp.concatenate(values, 1)),
+                update_split[:, start : start + 2 * BLOCK],
+            )
+            product = term if product is None else product + term
+        return weighted[level] - fold(product, sides, pivots)
+
+    def own_core(key):
+        return [gather_buffer[key][core * group + block] for block in range(group)]
+
+    weighted = []
+    prepare(1)
+    prepare_update(1)
+    fetch_lists([0], True)
+    cross_start()
+    gather_finish(("rhs", 0))
+    solved = fold(known_part(0), sides, pivots)
+    sent_up(solved, 0)
+    rhs_beside(1)
+    rhs_beside(2)
+    cross_spread()
+    fetch_lists(list(range(1, LEVELS - 1)), False)
+    coefficients = pivot_coefficients()
+    weighted.append(pivot_solve(solved, 0, *coefficients))
+    total = scatter_finish(("up", 0))
+    gather_buffer["up", 0][rank(1)] = total
+    gather_start(("up", 0))
+    rhs_deep(2)
+    rhs_relay(1)
+    prepare(2)
+    prepare_update(2)
+    rhs_finish(1)
+    known = known_part(1)
+    sent_up(fold(known, sides, pivots), 1)
+    low_start()
+    scatter_middle(("up", 1))
+    top_first()
+    gather_forward(("up", 0))
+    cross_share()
+    total = scatter_finish(("up", 1))
+    cross_rows()
+    total = total - fold(
+        along_columns(
+            rows_of(jnp.concatenate(own_core(("up", 0)), 1)), cross_row_split[...]
+        ),
+        half,
+        pivots,
+    )
+    gather_buffer["up", 1][rank(2)] = total
+    gather_start(("up", 1))
+    top_second()
+    gather_finish(("up", 0))
+    solved = fold(less_children(known, 1), sides, pivots)
+    weighted.append(pivot_solve(solved, 1, *coefficients))
+    rhs_relay(2)
+    rhs_finish(2)
+    product = known_part(2)
+    gather_forward(("up", 1))
+    prepare(3)
+
+    for level in range(2, LEVELS):
+        below = level - 1
+        gather_finish(("up", below))
+        solved = fold(less_children(product, level), sides, pivots)
+        if level + 1 < LEVELS:
+            key = ("up", level)
+            sent_up(solved, level)
+            weighted.append(pivot_solve(solved, level, *coefficients))
+            scatter_middle(key)
+            cross_turn()
+            top_relay()
             total = scatter_finish(key)
-            gather_buffer[key][rank(level - 1)] = total
+            gather_buffer[key][rank(level + 1)] = total
             gather_start(key)
-            scatter_middle(out_key, later=True)
+            rhs_finish(level + 1)
+            low_spread()
+            sent_down(square_of(weighted[1]), 1)
+            product = known_part(level + 1)
+            scatter_middle(("down", 0))
+            gather_forward(key)
+        else:
+            weighted.append(pivot_solve(solved, level, *coefficients))
+
+    for level in range(LEVELS - 1, 1, -1):
+        target = weighted[level]
+        if level + 1 < LEVELS:
+            gather_finish(("down", level))
+            target = with_parent(level)
+        square = square_of(target)
+        key = ("down", level - 1)
+        out_key = ("out", level)
+        sent_down(square, level)
+        scatter_middle(key)
+        issue(SHARE)
+        if level == LEVELS - 1:
+            sent_out(square_of(weighted[0]), 0)
+        sent_out(square, level)
+        if level == 2:
+            cross_columns()
+            low_finish()
+            out_ref[0, 0, :, :pivots] = scatter_finish(("out", 0))
+            gather_buffer["down", 0][rank(0)] = scatter_finish(("down", 0))
+        total = scatter_finish(key)
+        gather_buffer[key][rank(level - 1)] = total
+        gather_start(key)
+        scatter_middle(out_key, later=True)
+        issue(SHARE if level > 2 else len(bulk))
+        gather_forward(key)
+        if level > 2:
             issue(SHARE)
-            gather_forward(key)
-            issue(SHARE)
-    issue(len(bulk))
-    for level in reversed(range(LEVELS)):
+
+    total = gather_buffer["down", 0][rank(0)]
+    for block, values in enumerate(own_core(("down", 1))):
+        total = total - across(square_of(values), cross_col_split[block], half)
+    gather_buffer["down", 0][rank(0)] = total
+    gather_start(("down", 0))
+    gather_finish(("down", 1))
+    sent_out(square_of(with_parent(1)), 1)
+    scatter_middle(("out", 1))
+    gather_finish(("down", 0))
+    buffer = gather_buffer["down", 0]
+    total = out_ref[0, 0, :, :pivots]
+    for index in range(block_count(0)):
+        low_slot, high_slot = block_at(buffer, 0, 0, index, False)
+        values = jnp.concatenate([buffer[low_slot], buffer[high_slot]], 0)
+        total = total - across(square_of(values), low_split[index], sides)
+    out_ref[0, 0, :, :pivots] = total
+    for level in range(LEVELS - 1, 0, -1):
         out_ref[0, 0, :, level * pivots : (level + 1) * pivots] = scatter_finish(("out", level))
     for item in sends:
         wait_send(*item)
+    for level in range(1, top):
+        rhs_drain(level)
+    top_drain()
 
 
 def per_device(*arguments):
@@ -566,6 +946,7 @@
     fronts = lax.axis_size("front")
     plan = Plan(fronts, sides)
     nx = fronts // 2
+    group, wide = nx << 1, nx
     targets = jax.ShapeDtypeStruct((8, BLOCK), jnp.int32)
     buffers = []
     for level, rows in plan.gathers.values():
@@ -580,7 +961,7 @@
     dma = pltpu.SemaphoreType.DMA
     return pl.pallas_call(
         functools.partial(kernel, plan, pivots),
-        out_shape=jax.ShapeDtypeStruct(right_side.shape, F32),
+        out_shape=pltpu.VMEM(right_side.shape, F32),
         in_specs=[vmem, hbm, hbm, vmem, vmem, vmem, vmem],
         out_specs=vmem,
         scratch_shapes=[
@@ -598,6 +979,21 @@
             dma((len(plan.gathers), 2)),
             dma((len(plan.scatters), 2)),
             dma((len(plan.scatters), 2)),
+            dma((LEVELS, 4)),
+            dma((LEVELS, 4)),
+            dma((6,)),
+            dma((6,)),
+            pltpu.VMEM((2, group, wide, pivots, pivots), F32),
+            pltpu.VMEM((group, wide, pivots, pivots), F32),
+            pltpu.VMEM((group - 1, wide, pivots, pivots), F32),
+            pltpu.VMEM((group, pivots, pivots), F32),
+            pltpu.VMEM((group, pivots, pivots), F32),
+            pltpu.VMEM((2 * pivots, group * pivots), BF16),
+            pltpu.VMEM((group, 2 * pivots, pivots), BF16),
+            pltpu.VMEM((2, nx, nx, pivots, pivots), F32),
+            pltpu.VMEM((nx, nx, pivots, pivots), F32),
+            pltpu.VMEM((nx - 1, nx, pivots, pivots), F32),
+            pltpu.VMEM((nx, 2 * pivots, pivots), BF16),
             *buffers,
         ],
         compiler_params=pltpu.CompilerParams(collective_id=0, has_side_effects=True),

time: 103 us -> 92.5 us (0.90)
  Pallas kernels: 101 us -> 91.7 us
    pallas_call x1, Pallas kernels: 101 us -> 91.7 us  [per_device(): pl.pallas_call(functools.partial(kernel, plan, pivots), out_shape=pltpu.V...]
where the time goes in v1:
time: 92.5 us; the launch traced here: 92.4 us
  Pallas kernels  91.7 us (99%)
    pallas_call x1, Pallas kernels, per_device(): pl.pallas_call(functools.partial(kernel, plan, pivots), out_shape=pltpu.V...  91.7 us

profile of v1, /device:TPU:0, one launch (start us, length us, event | category | flops | bytes accessed | tf_op | source)
XLA Modules:
  0.0 92.4 jit_solution(4050948118114146208)
XLA Ops:
  0.0 91.7 %shard_map.73 = f32[1,1,96,512]{3,2,1,0:T(8,128)S(1)} custom-call(f32[1,1,96,512]{3,2,1,0:T(8,128)} %refs_0_.1, f32[1,1,128,7680]{3,2,1,0:T(8,128)} %refs_1_.1, f32[1,1,128,1792]{3,2,1,0:T(8,128)} %refs_2_.1, s32[1,14]{1,0:T(1,128)} %refs_3_.1, s32[1,1,256]{2,1,0:T(1,128)} %refs_4_.1, f32[1,1,512]{2,1,0:T(1,128)} %refs_5_.1, f32[1,1,256]{2,1,0:T(1,128)} %refs_6_.1), custom_call_target="tpu_custom_call" | custom-call | tf_op jit(solution)/shard_map/pallas_call | solution.py:962
  91.7 0.7 copy.9

commit v2 on v0

v2 whole, which is shorter than its diff:
```python
import functools

import jax
import jax.numpy as jnp
from jax import lax
from jax.experimental import pallas as pl
from jax.experimental.pallas import tpu as pltpu
from jax.sharding import PartitionSpec as P

LEVELS = 4
BLOCK = 128
TOP = LEVELS - 1
DEPTH = 1 << TOP - 1
MESH = pl.DeviceIdType.MESH
F32 = jnp.float32
BF16 = jnp.bfloat16


def flip(value, mask):
    result = value
    bit = 0
    while mask >> bit:
        if mask >> bit & 1:
            unit = 1 << bit
            result = result + (1 - 2 * lax.rem(lax.div(value, unit), 2)) * unit
        bit += 1
    return result


def split(values):
    high = values.astype(BF16)
    return high, (values - high.astype(F32)).astype(BF16)


def rows_of(values):
    high, low = split(values)
    return jnp.concatenate([high, low], 0)


def square_of(values):
    rows = rows_of(values)
    pieces = []
    for start in range(0, rows.shape[1], BLOCK):
        pieces += [rows[:, start : start + BLOCK]] * 2
    return jnp.concatenate(pieces, 1)


def along_columns(stacked, matrix):
    return lax.dot_general(
        stacked, matrix, (((1,), (1,)), ((), ())), preferred_element_type=F32
    )


def fold(product):
    sides = product.shape[0] // 2
    both = product[:sides] + product[sides:]
    pieces = []
    for start in range(0, both.shape[1], 2 * BLOCK):
        pieces.append(
            both[:, start : start + BLOCK] + both[:, start + BLOCK : start + 2 * BLOCK]
        )
    return jnp.concatenate(pieces, 1)


def across(square, matrix):
    product = jnp.dot(square, matrix, preferred_element_type=F32)
    half = product.shape[0] // 2
    return product[:half] + product[half:]


def far_first(count):
    return sorted(range(1, count), key=lambda mask: -bin(mask).count("1"))


def kernel(nx, pivots, keys, *refs):
    (
        rhs_ref,
        inverse_hbm,
        update_hbm,
        lists_ref,
        pairs_ref,
        diagonal_ref,
        coupling_ref,
        out_ref,
        inverse_raw,
        update_raw,
        inverse_split,
        update_split,
        coefficients,
        targets_ref,
        targets_far,
        targets_smem,
        result_near,
        result_far,
        cross_part,
        cross_landed,
        cross_row,
        cross_col,
        cross_row_split,
        cross_col_split,
        low_part,
        low_landed,
        low_sum,
        low_split,
        load_sem,
        targets_send,
        targets_recv,
        weight_send,
        weight_recv,
        side_send,
        side_recv,
        rhs_send,
        rhs_recv,
        out_send,
        out_recv,
        swap_send,
        swap_recv,
        gather_send,
        gather_recv,
        scatter_send,
        scatter_recv,
        *buffers,
    ) = refs
    half = rhs_ref.shape[2] // 2
    leaf = lax.axis_index("leaf")
    front = lax.axis_index("front")
    core, column = lax.rem(front, 2), lax.div(front, 2)
    row = lax.rem(leaf, 2)
    buffers = list(buffers)
    rhs = [buffers.pop(0) for _ in range(LEVELS)]
    out_part = [buffers.pop(0) for _ in range(LEVELS)]
    out_landed = [buffers.pop(0) for _ in range(LEVELS)]
    gathered, part, landed = {}, {}, {}
    for key in keys:
        gathered[key] = buffers.pop(0)
        part[key] = buffers.pop(0)
        landed[key] = buffers.pop(0)

    def chips(level):
        return nx << level

    def rank(level):
        return column * (1 << level) + lax.rem(leaf, 1 << level)

    def peer(level, mask, other_core=False):
        near = 1 - core if other_core else core
        return flip(leaf, mask % (1 << level)), flip(column, (mask >> level) % nx) * 2 + near

    partner = (leaf, column * 2 + 1 - core)

    def slot_at(level, child, block):
        slot_column, offset = divmod(block, 1 << level)
        return (slot_column << level + 1) + (child << level) + offset

    def slot(level):
        inside = lax.rem(leaf, 1 << level)
        if level == TOP:
            return (row * nx + column) * DEPTH + lax.div(inside, 2)
        if level < 2:
            return rank(level)
        return lax.div(inside, 2) * (2 * nx) + column * 2 + row

    def slot_place(level, index):
        if level == TOP:
            rest, deep = divmod(index, DEPTH)
            slot_row, slot_column = divmod(rest, nx)
        elif level < 2:
            slot_column, offset = divmod(index, 1 << level)
            deep, slot_row = divmod(offset, 2)
        else:
            deep, rest = divmod(index, 2 * nx)
            slot_column, slot_row = divmod(rest, 2)
        return slot_column, deep * 2 + slot_row

    def slot_blocks(level, index):
        slot_column, offset = slot_place(level, index)
        first = column_start(level) // BLOCK
        return [first + ((slot_column * 2 + parity) << level) + offset for parity in range(2)]

    def column_start(level):
        return 2 * nx * pivots * ((1 << level) - 1)

    def update_start(level):
        return 2 * pivots * ((1 << level) - 1)

    def block_count(level):
        return 2 * pivots * (1 << level) // BLOCK

    sends = []

    def send(source, target, sems, device):
        pltpu.make_async_remote_copy(
            source, target, *sems, device_id=device, device_id_type=MESH
        ).start()

    def span_copy(buffer, count, sems):
        span = buffer.at[pl.ds(0, count)]
        return pltpu.make_async_remote_copy(
            span, span, *sems, device_id=partner, device_id_type=MESH
        )

    def wait_recv(buffer, count, sems):
        span_copy(buffer, count, sems).wait_recv()

    def wait_send(buffer, count, sems):
        span_copy(buffer, count, sems).wait_send()

    def on(slot_column, slot_core=None):
        if slot_core is None:
            return pl.when(column == slot_column)
        return pl.when((column == slot_column) & (core == slot_core))

    def for_column(body):
        for index in range(nx):

            @on(index)
            def _():
                body(index)

    loads = []
    for level in range(LEVELS):
        cols = pl.ds(column_start(level), column_start(level + 1) - column_start(level))
        loads.append(
            pltpu.make_async_copy(
                inverse_hbm.at[0, 0, :, cols], inverse_raw.at[core, :, cols], load_sem.at[level]
            )
        )
    loads.append(
        pltpu.make_async_copy(update_hbm.at[0, 0], update_raw.at[core], load_sem.at[LEVELS])
    )
    for index in (0, LEVELS, *range(1, LEVELS)):
        loads[index].start()

    mine = pl.ds(core * half, half)
    theirs = pl.ds((1 - core) * half, half)

    def level_cols(level):
        return slice(level * pivots, (level + 1) * pivots)

    for level in range(LEVELS):
        rhs[level][slot(level), core] = rhs_ref[0, 0, mine, level_cols(level)]

    @on(0)
    def _():
        zeros = jnp.zeros((2, half, pivots), F32)
        for level in range(1, LEVELS):
            for index in range(chips(level)):
                if slot_place(level, index)[0]:
                    rhs[level][index] = zeros

    @on(1)
    def _():
        zeros = jnp.zeros((2, half, pivots), F32)
        for level in range(2):
            for place in range((1 << level) - 1, chips(level) - 1):
                out_landed[level][place] = zeros

    targets_ref[...] = jnp.zeros_like(targets_ref)
    targets_ref[:1, : lists_ref.shape[1]] = lists_ref[...]

    def swap(values):
        width = values.shape[1]
        even = lax.rem(lax.broadcasted_iota(jnp.int32, values.shape, 1), 2) == 0
        return jnp.where(
            even, pltpu.roll(values, width - 1, 1), pltpu.roll(values, 1, 1)
        )

    def pivot_coefficients():
        width = diagonal_ref.shape[2]
        from_pair = (
            lax.div(lax.broadcasted_iota(jnp.int32, (width // 2, width), 1), 2)
            == lax.broadcasted_iota(jnp.int32, (width // 2, width), 0)
        ).astype(F32)
        pair_rows = jnp.concatenate(
            [
                jnp.broadcast_to(coupling_ref[0], (8, width // 2)),
                jnp.broadcast_to(pairs_ref[0].astype(F32), (8, width // 2)),
            ],
            0,
        )
        repeated = jnp.dot(
            pair_rows, from_pair, precision=lax.Precision.HIGHEST, preferred_element_type=F32
        )
        couple, flags = repeated[:8], repeated[8:] > 0.5
        diagonal = jnp.broadcast_to(diagonal_ref[0], (8, width))

        other_diagonal = swap(diagonal)
        determinant = diagonal * other_diagonal - couple * couple
        straight = jnp.where(flags, other_diagonal / determinant, 1.0 / diagonal)
        crossed = jnp.where(flags, -couple / determinant, 0.0)
        coefficients[core, 0] = straight
        coefficients[core, 1] = crossed

    def pivot_solve(solved, level):
        straight, crossed = [
            jnp.concatenate(
                [coefficients[parity, kind, :1, level_cols(level)] for parity in range(2)], 1
            )
            for kind in range(2)
        ]
        return solved * straight + swap(solved) * crossed

    barrier = pltpu.get_barrier_semaphore()
    everyone = [
        (flip(leaf, mask % (2 * DEPTH)), flip(front, mask // (2 * DEPTH)))
        for mask in range(1, 4 * nx * DEPTH)
    ]
    for device in everyone:
        pl.semaphore_signal(barrier, inc=1, device_id=device, device_id_type=MESH)
    pivot_coefficients()
    pl.semaphore_wait(barrier, len(everyone))

    def list_sems(level):
        return targets_send.at[level], targets_recv.at[level]

    def list_copy(level):
        return pltpu.make_async_remote_copy(
            targets_ref,
            targets_far.at[level],
            *list_sems(level),
            device_id=(flip(leaf, 1 << level), front),
            device_id_type=MESH,
        )

    def rhs_sems(level, phase):
        return rhs_send.at[level, phase], rhs_recv.at[level, phase]

    def weight_sems(index):
        return weight_send.at[index], weight_recv.at[index]

    def rhs_base():
        sems = rhs_sems(0, 0)
        target = rhs[0].at[column, core]
        source = rhs_ref.at[0, 0]
        for mask in range(1, nx):
            for each, there in ((mine, core), (theirs, 1 - core)):
                send(
                    source.at[each, pl.ds(0, pivots)],
                    target,
                    sems,
                    (leaf, flip(column, mask) * 2 + there),
                )
        send(source.at[theirs, pl.ds(0, pivots)], target, sems, partner)
        sends.append((rhs[0].at[0], 1, sems))
        sends.append((rhs[0], nx - 1, sems))

    def rhs_halves():
        for level in range(1, LEVELS):
            send(
                rhs_ref.at[0, 0, theirs, pl.ds(level * pivots, pivots)],
                rhs[level].at[slot(level), core],
                rhs_sems(level, 3),
                partner,
            )
            sends.append((rhs[level].at[0], 1, rhs_sems(level, 3)))

    def give_inverse(level):
        loads[level].wait()
        cols = pl.ds(column_start(level), column_start(level + 1) - column_start(level))
        span = inverse_raw.at[core, :, cols]
        copy = pltpu.make_async_remote_copy(
            span, span, *weight_sems(level), device_id=partner, device_id_type=MESH
        )
        copy.start()
        return copy

    def give_update(level):
        if not level:
            loads[LEVELS].wait()
        cols = pl.ds(update_start(level), update_start(level + 1) - update_start(level))
        span = update_raw.at[core, :, cols]
        copy = pltpu.make_async_remote_copy(
            span, span, *weight_sems(LEVELS + level), device_id=partner, device_id_type=MESH
        )
        copy.start()
        return copy

    list_copies = [list_copy(level) for level in range(LEVELS - 1)]
    rhs_base()
    for copy in list_copies:
        copy.start()
    rhs_halves()
    given, given_update = {}, {}
    given[0] = give_inverse(0)
    given_update[0] = give_update(0)
    given[1] = give_inverse(1)
    given_update[1] = give_update(1)
    coefficient_copy = pltpu.make_async_remote_copy(
        coefficients.at[core],
        coefficients.at[core],
        *weight_sems(2 * LEVELS),
        device_id=partner,
        device_id_type=MESH,
    )
    coefficient_copy.start()
    given[2] = give_inverse(2)
    given_update[2] = give_update(2)
    given[3] = give_inverse(3)

    def prepare(level):
        given[level].wait_recv()
        for block in range(column_start(level) // BLOCK, column_start(level + 1) // BLOCK):
            for parity in range(2):
                high, low = split(inverse_raw[parity, :, block * BLOCK : (block + 1) * BLOCK])
                start = parity * 2 * pivots
                inverse_split[block, start : start + pivots] = high
                inverse_split[block, start + pivots : start + 2 * pivots] = low

    def prepare_update(level):
        given_update[level].wait_recv()
        cols = slice(update_start(level), update_start(level + 1))
        for parity in range(2):
            high, low = split(update_raw[parity, :, cols])
            start = parity * 2 * pivots
            update_split[start : start + pivots, cols] = high
            update_split[start + pivots : start + 2 * pivots, cols] = low

    def fetch_lists(levels, own):
        for level in levels:
            list_copies[level].wait()
        lists = [(targets_ref, 0)] if own else []
        lists += [(targets_far.at[level], level + 1) for level in levels]
        copies = [
            pltpu.make_async_copy(source, targets_smem.at[index], load_sem.at[LEVELS + 1 + index])
            for source, index in lists
        ]
        for copy in copies:
            copy.start()
        for copy in copies:
            copy.wait()

    def half_ready(level):
        wait_recv(rhs[level].at[0], 1, rhs_sems(level, 3))

    def base_ready():
        wait_recv(rhs[0].reshape(nx * 2, half, pivots), 2 * nx - 1, rhs_sems(0, 0))

    def one_across():
        half_ready(1)

        @on(0)
        def _():
            each = rhs[1].at[rank(1)]
            send(each, each, rhs_sems(1, 0), peer(1, 2))

    def one_beside():
        def body(index):
            if index:
                wait_recv(rhs[1], index, rhs_sems(1, 0))
            for back in range(index + 1):
                each = rhs[1].at[rank(1) - 2 * back]
                send(each, each, rhs_sems(1, 1), peer(1, 1))

        for_column(body)

    def one_ready():
        for_column(lambda index: wait_recv(rhs[1], index + 1, rhs_sems(1, 1)))

    def pair_start():
        return lax.rem(lax.div(leaf, 2), 2) * (2 * nx)

    def two_beside():
        half_ready(2)
        each = rhs[2].at[slot(2)]
        send(each, each, rhs_sems(2, 1), peer(2, 1))
        sends.append((rhs[2], 1, rhs_sems(2, 1)))

    def two_across():
        wait_recv(rhs[2], 1, rhs_sems(2, 1))

        @on(0)
        def _():
            span = rhs[2].at[pl.ds(pair_start(), 2)]
            send(span, span, rhs_sems(2, 0), peer(2, 4))

    def two_deep():
        def body(index):
            if index:
                wait_recv(rhs[2], 2 * index, rhs_sems(2, 0))
            span = rhs[2].at[pl.ds(pair_start(), 2 * (index + 1))]
            send(span, span, rhs_sems(2, 2), peer(2, 2))

        for_column(body)

    def two_ready():
        for_column(lambda index: wait_recv(rhs[2], 2 * (index + 1), rhs_sems(2, 2)))

    def top_run(slot_row, slot_column):
        return rhs[TOP].at[pl.ds((slot_row * nx + slot_column) * DEPTH, DEPTH)]

    def top_deep():
        half_ready(TOP)
        each = rhs[TOP].at[slot(TOP)]
        for deep in range(DEPTH - 1, 0, -1):
            send(each, each, rhs_sems(TOP, 0), peer(TOP, 2 * deep))
        sends.append((rhs[TOP], DEPTH - 1, rhs_sems(TOP, 0)))

    def top_beside():
        run = top_run(row, column)
        send(run, run, rhs_sems(TOP, 2), peer(TOP, 1))

    def top_first():
        wait_recv(rhs[TOP], DEPTH - 1, rhs_sems(TOP, 0))

        @pl.when(core == 1)
        def _():
            top_beside()

        @on(0, 0)
        def _():
            run = top_run(row, 0)
            send(run, run, rhs_sems(TOP, 1), peer(TOP, 1 << TOP))

        sends.append((rhs[TOP], DEPTH, rhs_sems(TOP, 2)))

    def top_second():
        @pl.when(core == 0)
        def _():
            top_beside()

        @on(0, 1)
        def _():
            wait_recv(rhs[TOP], DEPTH, rhs_sems(TOP, 2))
            for each in range(2):
                run = top_run(each, 0)
                send(run, run, rhs_sems(TOP, 1), peer(TOP, 1 << TOP))

        @on(1, 0)
        def _():
            wait_recv(rhs[TOP], DEPTH, rhs_sems(TOP, 1))
            run = top_run(row, 0)
            send(run, run, rhs_sems(TOP, 2), peer(TOP, 1))

    def top_ready():
        @on(0, 0)
        def _():
            wait_recv(rhs[TOP], DEPTH, rhs_sems(TOP, 2))

        @on(1, 0)
        def _():
            wait_recv(rhs[TOP], 2 * DEPTH, rhs_sems(TOP, 2))

        @on(1, 1)
        def _():
            wait_recv(rhs[TOP], DEPTH, rhs_sems(TOP, 2))
            wait_recv(rhs[TOP], 2 * DEPTH, rhs_sems(TOP, 1))

    def rhs_drain():
        def body(index):
            if not index:
                wait_send(rhs[1], 1, rhs_sems(1, 0))
                wait_send(rhs[2], 2, rhs_sems(2, 0))
            wait_send(rhs[1], index + 1, rhs_sems(1, 1))
            wait_send(rhs[2], 2 * (index + 1), rhs_sems(2, 2))

        for_column(body)

        @on(0, 0)
        def _():
            wait_send(rhs[TOP], DEPTH, rhs_sems(TOP, 1))

        @on(0, 1)
        def _():
            wait_send(rhs[TOP], 2 * DEPTH, rhs_sems(TOP, 1))

        @on(1, 0)
        def _():
            wait_send(rhs[TOP], DEPTH, rhs_sems(TOP, 2))

    def group_of(key):
        return key[1] + (1 if key[0] == "up" else 0), key[1] + (0 if key[0] == "up" else 1)

    def key_sems(kind, key):
        index = keys.index(key)
        if kind == "gather":
            return gather_send.at[index], gather_recv.at[index]
        return scatter_send.at[index], scatter_recv.at[index]

    def gather_start(key, total):
        level, _ = group_of(key)
        buffer, sems = gathered[key], key_sems("gather", key)
        buffer[rank(level)] = total
        for mask in far_first(chips(level)):
            each = buffer.at[rank(level)]
            send(each, each, sems, peer(level, mask))
        sends.append((buffer, chips(level) - 1, sems))

    def gather_finish(key):
        level, _ = group_of(key)
        wait_recv(gathered[key], chips(level) - 1, key_sems("gather", key))

    def scatter_start(key):
        _, level = group_of(key)
        sems = key_sems("scatter", key)
        for mask in far_first(chips(level)):
            send(
                part[key].at[flip(rank(level), mask)],
                landed[key].at[mask - 1],
                sems,
                peer(level, mask),
            )
        sends.append((part[key], chips(level) - 1, sems))

    def scatter_finish(key):
        _, level = group_of(key)
        wait_recv(landed[key], chips(level) - 1, key_sems("scatter", key))
        total = part[key][rank(level)]
        for place in range(chips(level) - 1):
            total = total + landed[key][place]
        return total

    def chosen_columns(level, child, index):
        place = update_start(level) // BLOCK + index
        upper = lax.rem(lax.div(leaf, 1 << level), 2)
        near, far = targets_smem[0, 0, place], targets_smem[level + 1, 0, place]
        block = near + (far - near) * (upper + child - 2 * upper * child)
        return inverse_split[column_start(level + 1) // BLOCK + block]

    def known_part(level):
        product = None
        for index in range(chips(level)):
            values = jnp.concatenate([rhs[level][index, parity] for parity in range(2)], 1)
            matrix = jnp.concatenate(
                [inverse_split[block] for block in slot_blocks(level, index)], 1
            )
            term = along_columns(rows_of(values), matrix)
            product = term if product is None else product + term
        return product

    def sent_up(solved, level):
        start, blocks = update_start(level), block_count(level)
        partial = across(square_of(solved), update_split[:, start : start + blocks * BLOCK])
        for block in range(blocks):
            part["up", level][block] = partial[:, block * BLOCK : (block + 1) * BLOCK]
        scatter_start(("up", level))

    def less_children(product, level):
        below = level - 1
        buffer = gathered["up", below]
        for child in range(2):
            for index in range(0, block_count(below), 2):
                pair = (index, index + 1)
                values = [buffer[slot_at(below, child, i)] for i in pair]
                matrices = [chosen_columns(below, child, i) for i in pair]
                product = product - along_columns(
                    rows_of(jnp.concatenate(values, 1)), jnp.concatenate(matrices, 1)
                )
        return product

    def sent_down(square, level):
        key = ("down", level - 1)
        for child in range(2):
            for index in range(0, block_count(level - 1), 2):
                pair = (index, index + 1)
                matrix = jnp.concatenate(
                    [chosen_columns(level - 1, child, i) for i in pair], 1
                )
                partial = across(square, matrix)
                for j, i in enumerate(pair):
                    part[key][slot_at(level - 1, child, i)] = partial[
                        :, j * BLOCK : (j + 1) * BLOCK
                    ]
        scatter_start(key)

    def with_parent(level):
        buffer = gathered["down", level]
        product = None
        for index in range(0, block_count(level), 2):
            values = jnp.concatenate([buffer[index], buffer[index + 1]], 1)
            start = update_start(level) + index * BLOCK
            term = along_columns(rows_of(values), update_split[:, start : start + 2 * BLOCK])
            product = term if product is None else product + term
        return weighted[level] - fold(product)

    def out_sems(level, phase):
        return out_send.at[level, phase], out_recv.at[level, phase]

    def made_out(square, level):
        for index in range(chips(level)):
            matrix = jnp.concatenate(
                [inverse_split[block] for block in slot_blocks(level, index)], 1
            )
            partial = across(square, matrix)
            for parity in range(2):
                out_part[level][index, parity] = partial[
                    :, parity * pivots : (parity + 1) * pivots
                ]

    def plain_out_start(level):
        sems = out_sems(level, 0)

        def one(mask):
            send(
                out_part[level].at[flip(rank(level), mask)],
                out_landed[level].at[mask - 1],
                sems,
                peer(level, mask),
            )

        @on(1)
        def _():
            for mask in far_first(chips(level)):
                if mask >> level:
                    one(mask)

        for mask in far_first(1 << level):
            one(mask)

    def plain_out_finish(level):
        def body(index):
            fewer = chips(level) if index == 0 else 1 << level
            if fewer > 1:
                wait_recv(out_landed[level], fewer - 1, out_sems(level, 0))

        for_column(body)
        total = out_part[level][rank(level)]
        for place in range(chips(level) - 1):
            total = total + out_landed[level][place]
        return total

    def plain_out_drain(level):
        def body(index):
            fewer = chips(level) if index else 1 << level
            if fewer > 1:
                wait_send(out_landed[level], fewer - 1, out_sems(level, 0))

        for_column(body)

    def out_add(level, start, place, count):
        span = pl.ds(start, count)
        out_part[level][span] = out_part[level][span] + out_landed[level][place : place + count]

    def middle_first():
        other = (1 - lax.rem(lax.div(leaf, 2), 2)) * (2 * nx)

        def body(index):
            each = 2 * (index + 1)
            send(
                out_part[2].at[pl.ds(other, each)],
                out_landed[2].at[pl.ds(0, each)],
                out_sems(2, 0),
                peer(2, 2),
            )

        for_column(body)

    def middle_second():
        def body(index):
            each = 2 * (index + 1)
            wait_recv(out_landed[2], each, out_sems(2, 0))
            out_add(2, pair_start(), 0, each)
            if index:
                send(
                    out_part[2].at[pl.ds(pair_start(), 2)],
                    out_landed[2].at[pl.ds(2 * nx, 2)],
                    out_sems(2, 1),
                    peer(2, 4),
                )

        for_column(body)

    def middle_third():
        @on(0)
        def _():
            wait_recv(out_landed[2], 2, out_sems(2, 1))
            out_add(2, pair_start(), 2 * nx, 2)

        send(
            out_part[2].at[pair_start() + column * 2 + (1 - row)],
            out_landed[2].at[2 * nx + 2],
            out_sems(2, 2),
            peer(2, 1),
        )
        sends.append((out_landed[2], 1, out_sems(2, 2)))

    def middle_finish():
        wait_recv(out_landed[2], 1, out_sems(2, 2))
        return out_part[2][slot(2)] + out_landed[2][2 * nx + 2]

    def middle_drain():
        def body(index):
            wait_send(out_landed[2], 2 * (index + 1), out_sems(2, 0))
            if index:
                wait_send(out_landed[2], 2, out_sems(2, 1))

        for_column(body)

    def final_index(slot_row, slot_column):
        return (slot_row * nx + slot_column) * DEPTH

    def final_run(slot_row, slot_column, count=1):
        return out_part[TOP].at[pl.ds(final_index(slot_row, slot_column), count * DEPTH)]

    def final_first():
        for index in range(nx):

            @on(index, 0)
            def _():
                send(
                    final_run(1 - row, 0, index + 1),
                    out_landed[TOP].at[pl.ds(0, (index + 1) * DEPTH)],
                    out_sems(TOP, 0),
                    peer(TOP, 1),
                )

        @on(1, 1)
        def _():
            for each in range(2):
                send(
                    final_run(each, 0),
                    out_landed[TOP].at[pl.ds(each * DEPTH, DEPTH)],
                    out_sems(TOP, 0),
                    peer(TOP, 1 << TOP),
                )

    def final_second():
        there = out_landed[TOP].at[pl.ds(2 * DEPTH, DEPTH)]
        for index in range(nx):

            @on(index, 0)
            def _():
                wait_recv(out_landed[TOP], (index + 1) * DEPTH, out_sems(TOP, 0))
                out_add(TOP, final_index(row, 0), 0, (index + 1) * DEPTH)

        @on(1, 0)
        def _():
            send(final_run(row, 0), there, out_sems(TOP, 1), peer(TOP, 1 << TOP))

        @on(0, 1)
        def _():
            wait_recv(out_landed[TOP], 2 * DEPTH, out_sems(TOP, 0))
            for each in range(2):
                out_add(TOP, final_index(each, 0), each * DEPTH, DEPTH)

        @pl.when(core == 1)
        def _():
            send(final_run(1 - row, column), there, out_sems(TOP, 1), peer(TOP, 1))

    def final_third():
        @pl.when((core == 1) | (column == 0))
        def _():
            wait_recv(out_landed[TOP], DEPTH, out_sems(TOP, 1))
            out_add(TOP, final_index(row, column), 2 * DEPTH, DEPTH)

        deep = lax.rem(lax.div(leaf, 2), DEPTH)
        for mask in range(DEPTH - 1, 0, -1):
            send(
                out_part[TOP].at[final_index(row, column) + flip(deep, mask)],
                out_landed[TOP].at[3 * DEPTH + mask - 1],
                out_sems(TOP, 2),
                peer(TOP, 2 * mask),
            )
        sends.append((out_landed[TOP], DEPTH - 1, out_sems(TOP, 2)))

    def final_finish():
        wait_recv(out_landed[TOP], DEPTH - 1, out_sems(TOP, 2))
        total = out_part[TOP][slot(TOP)]
        for place in range(DEPTH - 1):
            total = total + out_landed[TOP][3 * DEPTH + place]
        return total

    def final_drain():
        for index in range(nx):

            @on(index, 0)
            def _():
                wait_send(out_landed[TOP], (index + 1) * DEPTH, out_sems(TOP, 0))

        @on(1, 1)
        def _():
            wait_send(out_landed[TOP], 2 * DEPTH, out_sems(TOP, 0))

        @pl.when((core == 1) | (column == 1))
        def _():
            wait_send(out_landed[TOP], DEPTH, out_sems(TOP, 1))

    def swap_sems(level):
        return swap_send.at[level], swap_recv.at[level]

    def result_start(level, total):
        result_near[level] = total
        send(
            result_near.at[level, 1 - core], result_far.at[level], swap_sems(level), partner
        )
        sends.append((result_far, 1, swap_sems(level)))
        out_ref[0, 0, mine, level_cols(level)] = result_near[level, core]

    def result_finish(level):
        wait_recv(result_far, 1, swap_sems(level))
        out_ref[0, 0, theirs, level_cols(level)] = result_far[level]

    group, wide = chips(1), nx
    corner = rank(1)

    def side(index):
        return side_send.at[index], side_recv.at[index]

    def turned(level):
        cols = slice(update_start(level), update_start(level + 1))
        straight, crossed = [], []
        for parity in range(2):
            high, low = split(update_raw[parity, :, cols].T)
            straight += [high, low]
            crossed += [low, high]
        return jnp.concatenate(
            [jnp.concatenate(straight, 1), jnp.concatenate(crossed, 1)], 0
        )

    def cross_start():
        picks = [chosen_columns(0, child, core) for child in range(2)]
        product = across(turned(1), jnp.concatenate(picks, 1))
        for block in range(group):
            for i in range(wide):
                cross_part[block, i] = product[
                    block * pivots : (block + 1) * pivots, i * pivots : (i + 1) * pivots
                ]
        for mask in far_first(group):
            send(
                cross_part.at[flip(corner, mask)],
                cross_landed.at[mask - 1],
                side(1),
                peer(1, mask),
            )
        sends.append((cross_landed, group - 1, side(1)))

    def cross_share():
        wait_recv(cross_landed, group - 1, side(1))
        total = cross_part[corner]
        for place in range(group - 1):
            total = total + cross_landed[place]
        span = cross_row.at[pl.ds(core * wide, wide)]
        cross_row[pl.ds(core * wide, wide)] = total
        send(span, span, side(2), partner)
        sends.append((cross_row, wide, side(2)))

    def cross_rows():
        wait_recv(cross_row, wide, side(2))
        for block in range(group):
            cols = slice(block * pivots, (block + 1) * pivots)
            high, low = split(cross_row[block])
            cross_row_split[:pivots, cols] = high
            cross_row_split[pivots:, cols] = low

    def cross_turn():
        for mask in far_first(group):
            send(cross_row.at[flip(corner, mask)], cross_col.at[corner], side(3), peer(1, mask))
        sends.append((cross_row, group - 1, side(3)))
        cross_col[corner] = cross_row[corner]

    def cross_columns():
        wait_recv(cross_col, group - 1, side(3))
        for block in range(group):
            high, low = split(cross_col[block])
            cross_col_split[block, :pivots] = high
            cross_col_split[block, pivots:] = low

    def low_start():
        left = turned(0)
        for target in range(nx):
            product = across(left, inverse_split[target * 2 + core])
            for i in range(nx):
                low_part[target, i] = product[i * pivots : (i + 1) * pivots]

    def low_spread():
        @on(1)
        def _():
            send(low_part.at[0], low_landed, side(4), peer(0, 1))

    def low_share():
        @on(0)
        def _():
            wait_recv(low_landed, nx, side(4))
            low_part[0] = low_part[0] + low_landed[...]

        low_sum[core] = low_part[column]
        send(low_sum.at[core], low_sum.at[core], side(5), partner)
        sends.append((low_landed, nx, side(5)))

    def low_finish():
        wait_recv(low_landed, nx, side(5))
        for i in range(nx):
            for parity in range(2):
                cols = slice(parity * pivots, (parity + 1) * pivots)
                high, low = split(low_sum[parity, i])
                low_split[i, :pivots, cols] = high
                low_split[i, pivots:, cols] = low

    def low_drain():
        @on(1)
        def _():
            wait_send(low_landed, nx, side(4))

    weighted = []
    one_across()
    two_beside()
    top_deep()
    prepare(0)
    prepare_update(0)
    base_ready()
    solved = fold(known_part(0))
    sent_up(solved, 0)
    one_beside()
    fetch_lists([0], True)
    two_across()
    prepare(1)
    prepare_update(1)
    cross_start()
    total = scatter_finish(("up", 0))
    gather_start(("up", 0), total)
    one_ready()
    known = known_part(1)
    sent_up(fold(known), 1)
    top_first()
    two_deep()
    fetch_lists(list(range(1, LEVELS - 1)), False)
    prepare(2)
    prepare_update(2)
    coefficient_copy.wait_recv()
    weighted.append(pivot_solve(solved, 0))
    low_start()
    gather_finish(("up", 0))
    cross_share()
    total = scatter_finish(("up", 1))
    cross_rows()
    values = [gathered["up", 0][block] for block in range(group)]
    total = total - fold(
        along_columns(rows_of(jnp.concatenate(values, 1)), cross_row_split[...])
    )
    gather_start(("up", 1), total)
    low_spread()
    solved = fold(less_children(known, 1))
    weighted.append(pivot_solve(solved, 1))
    top_second()
    two_ready()
    product = known_part(2)
    prepare(3)
    gather_finish(("up", 1))
    solved = fold(less_children(product, 2))
    sent_up(solved, 2)
    weighted.append(pivot_solve(solved, 2))
    low_share()
    total = scatter_finish(("up", 2))
    gather_start(("up", 2), total)
    cross_turn()
    sent_down(square_of(weighted[1]), 1)
    top_ready()
    product = known_part(3)
    low_finish()
    cross_columns()
    gather_finish(("up", 2))
    solved = fold(less_children(product, 3))
    weighted.append(pivot_solve(solved, 3))

    square = square_of(weighted[3])
    sent_down(square, 3)
    made_out(square, 3)
    final_first()
    made_out(square_of(weighted[0]), 0)
    plain_out_start(0)
    small = scatter_finish(("down", 0))
    total = scatter_finish(("down", 2))
    gather_start(("down", 2), total)
    final_second()
    gather_finish(("down", 2))
    square = square_of(with_parent(2))
    sent_down(square, 2)
    made_out(square, 2)
    middle_first()
    final_third()
    base = plain_out_finish(0)
    total = scatter_finish(("down", 1))
    gather_start(("down", 1), total)
    middle_second()
    gather_finish(("down", 1))
    for block in range(group):
        small = small - across(square_of(gathered["down", 1][block]), cross_col_split[block])
    gather_start(("down", 0), small)
    made_out(square_of(with_parent(1)), 1)
    plain_out_start(1)
    result_start(3, final_finish())
    middle_third()
    gather_finish(("down", 0))
    base = jnp.concatenate([base[0], base[1]], 1)
    for block in range(block_count(0)):
        base = base - across(square_of(gathered["down", 0][block]), low_split[block])
    result_start(0, jnp.stack([base[:, :pivots], base[:, pivots:]]))
    result_start(2, middle_finish())
    result_start(1, plain_out_finish(1))
    for level in (3, 0, 2, 1):
        result_finish(level)
    for item in sends:
        wait_send(*item)
    rhs_drain()
    for level in range(2):
        plain_out_drain(level)
    middle_drain()
    final_drain()
    low_drain()
    for copy in [*given.values(), *given_update.values(), coefficient_copy]:
        copy.wait_send()


def per_device(*arguments):
    right_side, factor_inverse, update_panel = arguments[:3]
    pivots = factor_inverse.shape[2]
    half = right_side.shape[2] // 2
    nx = lax.axis_size("front") // 2
    keys = [(kind, level) for kind in ("up", "down") for level in range(LEVELS - 1)]
    targets = (8, BLOCK)
    group, wide = nx << 1, nx
    blocks = factor_inverse.shape[3] // BLOCK
    buffers = []
    for _ in range(2):
        buffers += [pltpu.VMEM((nx << level, 2, half, pivots), F32) for level in range(LEVELS)]
    buffers += [pltpu.VMEM((nx << level, 2, half, pivots), F32) for level in range(LEVELS)]
    for kind, level in keys:
        wider, narrower = (nx << level + 1, nx << level)
        first, second = (wider, narrower) if kind == "up" else (narrower, wider)
        buffers += [pltpu.VMEM((count, half, BLOCK), F32) for count in (first, second, second)]
    vmem = pl.BlockSpec(memory_space=pltpu.VMEM)
    hbm = pl.BlockSpec(memory_space=pl.ANY)
    dma = pltpu.SemaphoreType.DMA
    square = (pivots, pivots)
    return pl.pallas_call(
        functools.partial(kernel, nx, pivots, keys),
        out_shape=pltpu.VMEM(right_side.shape, F32),
        in_specs=[vmem, hbm, hbm, vmem, vmem, vmem, vmem],
        out_specs=vmem,
        scratch_shapes=[
            pltpu.VMEM((2,) + factor_inverse.shape[2:], F32),
            pltpu.VMEM((2,) + update_panel.shape[2:], F32),
            pltpu.VMEM((blocks, 4 * pivots, BLOCK), BF16),
            pltpu.VMEM((4 * pivots, update_panel.shape[3]), BF16),
            pltpu.VMEM((2, 2, 8, LEVELS * pivots), F32),
            pltpu.VMEM(targets, jnp.int32),
            pltpu.VMEM((LEVELS - 1,) + targets, jnp.int32),
            pltpu.SMEM((LEVELS,) + targets, jnp.int32),
            pltpu.VMEM((LEVELS, 2, half, pivots), F32),
            pltpu.VMEM((LEVELS, half, pivots), F32),
            pltpu.VMEM((group, wide) + square, F32),
            pltpu.VMEM((group - 1, wide) + square, F32),
            pltpu.VMEM((group,) + square, F32),
            pltpu.VMEM((group,) + square, F32),
            pltpu.VMEM((2 * pivots, group * pivots), BF16),
            pltpu.VMEM((group, 2 * pivots, pivots), BF16),
            pltpu.VMEM((nx, nx) + square, F32),
            pltpu.VMEM((nx,) + square, F32),
            pltpu.VMEM((2, nx) + square, F32),
            pltpu.VMEM((nx, 2 * pivots, 2 * pivots), BF16),
            dma((2 * LEVELS + 1,)),
            dma((LEVELS - 1,)),
            dma((LEVELS - 1,)),
            dma((2 * LEVELS + 1,)),
            dma((2 * LEVELS + 1,)),
            dma((6,)),
            dma((6,)),
            dma((LEVELS, 4)),
            dma((LEVELS, 4)),
            dma((LEVELS, 3)),
            dma((LEVELS, 3)),
            dma((LEVELS,)),
            dma((LEVELS,)),
            dma((len(keys),)),
            dma((len(keys),)),
            dma((len(keys),)),
            dma((len(keys),)),
            *buffers,
        ],
        compiler_params=pltpu.CompilerParams(collective_id=0, has_side_effects=True),
    )(*arguments)


def solution(mesh):
    in_specs = (
        P("leaf", "front", None, None),
        P("leaf", "front", None, None),
        P("leaf", "front", None, None),
        P("leaf", None),
        P("leaf", "front", None),
        P("leaf", "front", None),
        P("leaf", "front", None),
    )
    out_specs = P("leaf", "front", None, None)
    return jax.shard_map(
        per_device, mesh=mesh, in_specs=in_specs, out_specs=out_specs, check_vma=False
    )
```

time: 103 us -> 78.4 us (0.76)
  Pallas kernels: 101 us -> 77.6 us
    pallas_call x1, Pallas kernels: 101 us -> 77.6 us  [per_device(): pl.pallas_call(functools.partial(kernel, nx, pivots, keys), out_shape=plt...]
where the time goes in v2:
time: 78.4 us; the launch traced here: 78.3 us
  Pallas kernels  77.6 us (99%)
    pallas_call x1, Pallas kernels, per_device(): pl.pallas_call(functools.partial(kernel, nx, pivots, keys), out_shape=plt...  77.6 us

profile of v2, /device:TPU:0, one launch (start us, length us, event | category | flops | bytes accessed | tf_op | source)
XLA Modules:
  0.0 78.3 jit_solution(11337880006856875103)
XLA Ops:
  0.0 77.6 %shard_map.73 = f32[1,1,96,512]{3,2,1,0:T(8,128)S(1)} custom-call(f32[1,1,96,512]{3,2,1,0:T(8,128)} %refs_0_.1, f32[1,1,128,7680]{3,2,1,0:T(8,128)} %refs_1_.1, f32[1,1,128,1792]{3,2,1,0:T(8,128)} %refs_2_.1, s32[1,14]{1,0:T(1,128)} %refs_3_.1, s32[1,1,256]{2,1,0:T(1,128)} %refs_4_.1, f32[1,1,512]{2,1,0:T(1,128)} %refs_5_.1, f32[1,1,256]{2,1,0:T(1,128)} %refs_6_.1), custom_call_target="tpu_custom_call" | custom-call | tf_op jit(solution)/shard_map/pallas_call | solution.py:1124
  77.6 0.7 copy.9

commit v3 on v2

--- a/solution.py
+++ b/solution.py
@@ -69,7 +69,7 @@
 
 
 def far_first(count):
-    return sorted(range(1, count), key=lambda mask: -bin(mask).count("1"))
+    return sorted(range(1, count), key=lambda mask: (-(mask & DEPTH), -bin(mask).count("1")))
 
 
 def kernel(nx, pivots, keys, *refs):
@@ -254,6 +254,8 @@
         for level in range(2):
             for place in range((1 << level) - 1, chips(level) - 1):
                 out_landed[level][place] = zeros
+        for place in range(2):
+            out_landed[2][2 * nx + place] = zeros
 
     targets_ref[...] = jnp.zeros_like(targets_ref)
     targets_ref[:1, : lists_ref.shape[1]] = lists_ref[...]
@@ -745,43 +747,44 @@
         for_column(body)
 
     def middle_second():
+        here = pair_start() + row
+        beside = pair_start() + 1 - row
+
         def body(index):
             each = 2 * (index + 1)
             wait_recv(out_landed[2], each, out_sems(2, 0))
             out_add(2, pair_start(), 0, each)
             if index:
-                send(
-                    out_part[2].at[pl.ds(pair_start(), 2)],
-                    out_landed[2].at[pl.ds(2 * nx, 2)],
-                    out_sems(2, 1),
-                    peer(2, 4),
-                )
+                for place, source, mask in ((1, beside, 5), (0, here, 4)):
+                    send(
+                        out_part[2].at[source],
+                        out_landed[2].at[2 * nx + place],
+                        out_sems(2, 1),
+                        peer(2, mask),
+                    )
+            send(
+                out_part[2].at[beside + 2 * index],
+                out_landed[2].at[2 * nx + 2],
+                out_sems(2, 1),
+                peer(2, 1),
+            )
 
         for_column(body)
 
-    def middle_third():
-        @on(0)
-        def _():
-            wait_recv(out_landed[2], 2, out_sems(2, 1))
-            out_add(2, pair_start(), 2 * nx, 2)
-
-        send(
-            out_part[2].at[pair_start() + column * 2 + (1 - row)],
-            out_landed[2].at[2 * nx + 2],
-            out_sems(2, 2),
-            peer(2, 1),
-        )
-        sends.append((out_landed[2], 1, out_sems(2, 2)))
-
     def middle_finish():
-        wait_recv(out_landed[2], 1, out_sems(2, 2))
-        return out_part[2][slot(2)] + out_landed[2][2 * nx + 2]
+        def body(index):
+            wait_recv(out_landed[2], 1 if index else nx + 1, out_sems(2, 1))
+
+        for_column(body)
+        total = out_part[2][slot(2)]
+        for place in range(3):
+            total = total + out_landed[2][2 * nx + place]
+        return total
 
     def middle_drain():
         def body(index):
             wait_send(out_landed[2], 2 * (index + 1), out_sems(2, 0))
-            if index:
-                wait_send(out_landed[2], 2, out_sems(2, 1))
+            wait_send(out_landed[2], nx + 1 if index else 1, out_sems(2, 1))
 
         for_column(body)
 
@@ -1046,7 +1049,6 @@
     top_ready()
     product = known_part(3)
     low_finish()
-    cross_columns()
     gather_finish(("up", 2))
     solved = fold(less_children(product, 3))
     weighted.append(pivot_solve(solved, 3))
@@ -1057,6 +1059,7 @@
     final_first()
     made_out(square_of(weighted[0]), 0)
     plain_out_start(0)
+    cross_columns()
     small = scatter_finish(("down", 0))
     total = scatter_finish(("down", 2))
     gather_start(("down", 2), total)
@@ -1072,13 +1075,12 @@
     gather_start(("down", 1), total)
     middle_second()
     gather_finish(("down", 1))
+    made_out(square_of(with_parent(1)), 1)
+    plain_out_start(1)
     for block in range(group):
         small = small - across(square_of(gathered["down", 1][block]), cross_col_split[block])
     gather_start(("down", 0), small)
-    made_out(square_of(with_parent(1)), 1)
-    plain_out_start(1)
     result_start(3, final_finish())
-    middle_third()
     gather_finish(("down", 0))
     base = jnp.concatenate([base[0], base[1]], 1)
     for block in range(block_count(0)):

time: 78.4 us -> 77.8 us (level)
  no operation moved by 1% of the time
where the time goes in v3:
time: 77.8 us; the launch traced here: 77.7 us
  Pallas kernels  77 us (99%)
    pallas_call x1, Pallas kernels, per_device(): pl.pallas_call(functools.partial(kernel, nx, pivots, keys), out_shape=plt...  77 us

profile of v3, /device:TPU:0, one launch (start us, length us, event | category | flops | bytes accessed | tf_op | source)
XLA Modules:
  0.0 77.7 jit_solution(3081221711408158318)
XLA Ops:
  0.0 77.0 %shard_map.73 = f32[1,1,96,512]{3,2,1,0:T(8,128)S(1)} custom-call(f32[1,1,96,512]{3,2,1,0:T(8,128)} %refs_0_.1, f32[1,1,128,7680]{3,2,1,0:T(8,128)} %refs_1_.1, f32[1,1,128,1792]{3,2,1,0:T(8,128)} %refs_2_.1, s32[1,14]{1,0:T(1,128)} %refs_3_.1, s32[1,1,256]{2,1,0:T(1,128)} %refs_4_.1, f32[1,1,512]{2,1,0:T(1,128)} %refs_5_.1, f32[1,1,256]{2,1,0:T(1,128)} %refs_6_.1), custom_call_target="tpu_custom_call" | custom-call | tf_op jit(solution)/shard_map/pallas_call | solution.py:1126
  77.0 0.7 copy.9

commit v4 on v3

--- a/solution.py
+++ b/solution.py
@@ -309,7 +309,6 @@
     ]
     for device in everyone:
         pl.semaphore_signal(barrier, inc=1, device_id=device, device_id_type=MESH)
-    pivot_coefficients()
     pl.semaphore_wait(barrier, len(everyone))
 
     def list_sems(level):
@@ -387,6 +386,7 @@
     given_update[0] = give_update(0)
     given[1] = give_inverse(1)
     given_update[1] = give_update(1)
+    pivot_coefficients()
     coefficient_copy = pltpu.make_async_remote_copy(
         coefficients.at[core],
         coefficients.at[core],

time: 77.8 us -> 77.8 us (level)
  no operation moved by 1% of the time
where the time goes in v4:
time: 77.8 us; the launch traced here: 77.7 us
  Pallas kernels  77 us (99%)
    pallas_call x1, Pallas kernels, per_device(): pl.pallas_call(functools.partial(kernel, nx, pivots, keys), out_shape=plt...  77 us

profile of v4, /device:TPU:0, one launch (start us, length us, event | category | flops | bytes accessed | tf_op | source)
XLA Modules:
  0.0 77.7 jit_solution(5094470872284613517)
XLA Ops:
  0.0 77.0 %shard_map.73 = f32[1,1,96,512]{3,2,1,0:T(8,128)S(1)} custom-call(f32[1,1,96,512]{3,2,1,0:T(8,128)} %refs_0_.1, f32[1,1,128,7680]{3,2,1,0:T(8,128)} %refs_1_.1, f32[1,1,128,1792]{3,2,1,0:T(8,128)} %refs_2_.1, s32[1,14]{1,0:T(1,128)} %refs_3_.1, s32[1,1,256]{2,1,0:T(1,128)} %refs_4_.1, f32[1,1,512]{2,1,0:T(1,128)} %refs_5_.1, f32[1,1,256]{2,1,0:T(1,128)} %refs_6_.1), custom_call_target="tpu_custom_call" | custom-call | tf_op jit(solution)/shard_map/pallas_call | solution.py:1126
  77.0 0.7 copy.9
